TPU v7x, 512 devices: a whole 4x8x8 slice. The times are simulated.
512 devices in a mesh: dp: 32 (over y, x), mp: 16 (over z, core).
Axes of the slice: x: 4, y: 8, z: 8, core: 2. Of those that a mesh axis runs over, the one named last changes fastest.
Arguments:
- query_new: bfloat16 [512, 4096], P(('dp', 'mp')), parts along dimension 0, may hold values from -140 to 140
- key_new: bfloat16 [512, 1024], P(('dp', 'mp')), parts along dimension 0, may hold values from -5 to 5
- value_new: bfloat16 [512, 1024], P(('dp', 'mp')), parts along dimension 0, may hold values from -5 to 5
- prefix_keys: bfloat16 [65536, 1024], P(('dp', 'mp')), parts along dimension 0, may hold values from -5 to 5
- prefix_values: bfloat16 [65536, 1024], P(('dp', 'mp')), parts along dimension 0, may hold values from -5 to 5
- sample_suffix_keys: bfloat16 [512, 64, 1024], P(('dp', 'mp')), parts along dimension 0, may hold values from -5 to 5
- sample_suffix_values: bfloat16 [512, 64, 1024], P(('dp', 'mp')), parts along dimension 0, may hold values from -5 to 5
- prefix_len: int32 [32], P('dp'), parts along dimension 0, may hold values from 512 to 2048
- suffix_len: int32 [512], P(('dp', 'mp')), parts along dimension 0, may hold values from 1 to 64, as said below
- residual: bfloat16 [512, 8192], P(('dp', 'mp')), parts along dimension 0, may hold values from -3 to 3
- out_weight: bfloat16 [4096, 8192], P('mp'), may hold values from -0.1875 to 0.1875
- norm_gain: bfloat16 [8192], replicated, may hold values from 0.5 to 1.5
Outputs:
- hidden: bfloat16 [512, 8192], P(('dp', 'mp')), parts along dimension 0
- normed: bfloat16 [512, 8192], P(('dp', 'mp')), parts along dimension 0
There are 32 independent parts, one for each index of `dp`. A program takes and returns all parts, laid end to end along the dimension named above; an argument that names none is the same for every part. Nothing has to cross between parts.
Inputs may be any that keep to these rules, and one draw needn't show every extreme that they name: `suffix_len`: some sample has exactly 64 cached generated tokens.
All inputs are finite; a program needn't handle non-finite values.
Results may differ from a plain program's by a relative error of at most 0.0085.
Values may be sent and summed in bfloat16 or wider, within the bound.
A program may use at most 64 MiB of HBM per device.

v0:
```python
import jax
import jax.numpy as jnp
from jax import lax
from jax.sharding import PartitionSpec as P

HEAD_SIZE = 128
KEY_VALUE_HEADS = 8
HQ = 32


def joined_along(blocks, dim):
    blocks = jnp.moveaxis(blocks, 0, dim)
    shape = blocks.shape
    return blocks.reshape(*shape[:dim], shape[dim] * shape[dim + 1], *shape[dim + 2 :])


def from_everyone(value, axis):
    length = lax.axis_size(axis)
    return lax.all_to_all(
        jnp.broadcast_to(value[None], (length, *value.shape)), axis, 0, 0, tiled=True
    )


def gather_directly(value, axis, dim):
    return joined_along(from_everyone(value, axis), dim)


def of_everyone(value, axis):
    everything = from_everyone(value, axis)
    return jnp.max(everything, axis=0)


def cut_along(value, dim, length):
    before, after = (value.shape[:dim], value.shape[dim + 1 :])
    return jnp.moveaxis(value.reshape(*before, length, -1, *after), dim, 0)


def sent_and_summed(value, axis, dim):
    blocks = cut_along(value, dim, lax.axis_size(axis))
    arrived = lax.all_to_all(blocks, axis, split_axis=0, concat_axis=0, tiled=True)
    return arrived.sum(axis=0)


def sent_together(arrays, axis, dim, along):
    columns = [a.reshape(*a.shape[:along], -1) for a in arrays]
    both = jnp.concatenate(columns, axis=along)
    whole, at, outs = (sent_and_summed(both, axis, dim), 0, [])
    for a, column in zip(arrays, columns):
        share = whole[..., at : at + column.shape[along]]
        outs.append(share.reshape(*share.shape[:along], *a.shape[along:]))
        at += column.shape[along]
    return tuple(outs)


def local(
    query_new,
    key_new,
    value_new,
    prefix_keys,
    prefix_values,
    sample_suffix_keys,
    sample_suffix_values,
    prefix_len,
    suffix_len,
    residual,
    out_weight,
    norm_gain,
):
    count_mp = lax.axis_size("mp")
    place = lax.axis_index("mp")
    samples_per_part = query_new.shape[0]
    batch = samples_per_part * count_mp
    heads_dev = out_weight.shape[0] // HEAD_SIZE
    group = HQ // KEY_VALUE_HEADS
    pre_dev = prefix_keys.shape[0]
    suffix_result = sample_suffix_keys.shape[1]
    score_scale = HEAD_SIZE ** (-0.5)
    first_row = place * samples_per_part
    queries = gather_directly(query_new, "mp", 0)
    query_all = queries.reshape(batch, KEY_VALUE_HEADS, group, HEAD_SIZE)
    pkeys = prefix_keys.reshape(pre_dev, KEY_VALUE_HEADS, HEAD_SIZE)
    prefix_value_rows = prefix_values.reshape(pre_dev, KEY_VALUE_HEADS, HEAD_SIZE)
    s_pre = (
        jnp.einsum("bkgd,pkd->bkgp", query_all, pkeys, preferred_element_type=jnp.float32)
        * score_scale
    )
    positions = place * pre_dev + lax.iota(jnp.int32, pre_dev)
    pvalid = (positions < prefix_len[0])[None, None, None, :]
    s_pre = jnp.where(pvalid, s_pre, -jnp.inf)
    query_sample_rows = query_new.reshape(samples_per_part, KEY_VALUE_HEADS, group, HEAD_SIZE)
    suffix_key_rows = sample_suffix_keys.reshape(
        samples_per_part, suffix_result, KEY_VALUE_HEADS, HEAD_SIZE
    )
    suffix_value_rows = sample_suffix_values.reshape(
        samples_per_part, suffix_result, KEY_VALUE_HEADS, HEAD_SIZE
    )
    nvals = value_new.reshape(samples_per_part, KEY_VALUE_HEADS, HEAD_SIZE)
    suffix_score_rows = (
        jnp.einsum(
            "cqxt,caqt->cqxa",
            query_sample_rows,
            suffix_key_rows,
            preferred_element_type=jnp.float32,
        )
        * score_scale
    )
    svalid = (lax.iota(jnp.int32, suffix_result)[None, :] < suffix_len[:, None])[:, None, None, :]
    suffix_score_rows = jnp.where(svalid, suffix_score_rows, -jnp.inf)
    fresh_score_rows = (
        jnp.einsum(
            "exio,exo->exi",
            query_sample_rows,
            key_new.reshape(samples_per_part, KEY_VALUE_HEADS, HEAD_SIZE),
            preferred_element_type=jnp.float32,
        )
        * score_scale
    )
    top_pre = jnp.maximum(jnp.max(s_pre, -1), -1e30)
    own_top = lax.dynamic_slice_in_dim(top_pre, first_row, samples_per_part, 0)
    own_top = jnp.maximum(jnp.maximum(own_top, jnp.max(suffix_score_rows, -1)), fresh_score_rows)
    local_top = lax.dynamic_update_slice_in_dim(top_pre, own_top, first_row, 0)
    top = of_everyone(local_top, "mp")
    top_own = lax.dynamic_slice_in_dim(top, first_row, samples_per_part, 0)
    w_pre = jnp.where(pvalid, jnp.exp(s_pre - top[..., None]), 0.0)
    total = jnp.sum(w_pre, -1)
    summed_rows = jnp.einsum(
        "wnso,onr->wnsr",
        w_pre.astype(jnp.bfloat16),
        prefix_value_rows,
        preferred_element_type=jnp.float32,
    )
    suffix_weight_rows = jnp.where(svalid, jnp.exp(suffix_score_rows - top_own[..., None]), 0.0)
    w_new = jnp.exp(fresh_score_rows - top_own)
    own_total = jnp.sum(suffix_weight_rows, -1) + w_new
    own_sum = jnp.einsum(
        "cjax,cxjq->cjaq",
        suffix_weight_rows.astype(jnp.bfloat16),
        suffix_value_rows,
        preferred_element_type=jnp.float32,
    )
    own_sum = (
        own_sum
        + w_new.astype(jnp.bfloat16).astype(jnp.float32)[..., None]
        * nvals.astype(jnp.float32)[:, :, None, :]
    )
    total = lax.dynamic_update_slice_in_dim(
        total,
        lax.dynamic_slice_in_dim(total, first_row, samples_per_part, 0) + own_total,
        first_row,
        0,
    )
    summed_rows = lax.dynamic_update_slice_in_dim(
        summed_rows,
        lax.dynamic_slice_in_dim(summed_rows, first_row, samples_per_part, 0) + own_sum,
        first_row,
        0,
    )
    total_flat = total.reshape(batch, HQ)
    summed_flat = summed_rows.reshape(batch, HQ, HEAD_SIZE)
    mine_total, mine_summed = sent_together((total_flat, summed_flat), "mp", 1, 2)
    attn = (
        (mine_summed / mine_total[..., None])
        .astype(jnp.bfloat16)
        .reshape(batch, heads_dev * HEAD_SIZE)
    )
    proj = sent_and_summed(jnp.dot(attn, out_weight, preferred_element_type=jnp.float32), "mp", 0)
    stream = residual.astype(jnp.float32) + proj
    hidden = stream.astype(jnp.bfloat16)
    meansq = jnp.mean(stream * stream, axis=-1, keepdims=True)
    normed = (stream * lax.rsqrt(meansq + 1e-05) * norm_gain.astype(jnp.float32)[None, :]).astype(
        jnp.bfloat16
    )
    return (hidden, normed)


def solution(mesh):
    placed = (
        P(("dp", "mp"), None),
        P(("dp", "mp"), None),
        P(("dp", "mp"), None),
        P(("dp", "mp"), None),
        P(("dp", "mp"), None),
        P(("dp", "mp"), None, None),
        P(("dp", "mp"), None, None),
        P("dp"),
        P(("dp", "mp")),
        P(("dp", "mp"), None),
        P("mp", None),
        P(),
    )
    return jax.shard_map(
        local,
        mesh=mesh,
        in_specs=placed,
        out_specs=(P(("dp", "mp"), None), P(("dp", "mp"), None)),
        check_vma=False,
    )
```

profile of v0, /device:TPU:1, one launch (start us, length us, event | category | flops | bytes accessed | tf_op | source)
XLA Modules:
  0.0 88.9 jit_solution(17414631474509699725)
XLA Ops:
  0.7 0.8 reduce.6
  1.5 0.2 broadcast_in_dim.70
  1.7 0.5 broadcast.45
  2.2 1.4 %reduce.11 = bf16[16,4096]{1,0:T(8,128)(2,1)S(1)} reduce(bf16[16,1,4096]{2,1,0:T(2,128)(2,1)S(1)} %broadcast_in_dim.70, bf16[]{:T(256)} %broadcast.45), dimensions={1}, to_apply=%broadcast_in_dim.70.reduce_sub_computation | reduce | bytes 262146 | tf_op jit(solution)/shard_map/broadcast_in_dim | solution.py:20
  3.6 0.7 reshape.142
  4.3 11.8 %all-to-all-start = ((bf16[16,2,2048]{2,1,0:T(2,128)(2,1)}), bf16[16,2,2048]{2,1,0:T(2,128)(2,1)S(1)}, u32[]{:S(2)}, u32[]{:S(2)}) async-start(bf16[16,2,2048]{2,1,0:T(2,128)(2,1)} %reshape.142), calls=%async_computation | async-start | bytes 262144 | tf_op jit(solution)/shard_map/all_to_all | solution.py:19
  16.2 1.0 %copy.142 = bf16[16,8,8,128]{3,2,1,0:T(8,128)(2,1)S(1)} copy(bf16[16,8,8,128]{3,1,2,0:T(8,128)(2,1)} %bitcast.88) | data formatting | bytes 524288
  17.8 0.9 %copy.143 = bf16[8,8,8,128]{3,2,1,0:T(8,128)(2,1)S(1)} copy(bf16[8,8,8,128]{3,1,2,0:T(8,128)(2,1)} %bitcast.93) | data formatting | bytes 262144
  19.4 0.2 fusion.35
  19.7 0.1 copy.117
  19.7 0.1 fusion.26
  19.9 0.1 copy.133
  20.0 5.1 %all-to-all-done = bf16[16,2,2048]{2,1,0:T(2,128)(2,1)S(1)} async-done(((bf16[16,2,2048]{2,1,0:T(2,128)(2,1)}), bf16[16,2,2048]{2,1,0:T(2,128)(2,1)S(1)}, u32[]{:S(2)}, u32[]{:S(2)}) %all-to-all-start) | async-done | bytes 131104 | tf_op jit(solution)/shard_map/all_to_all | solution.py:19
  25.1 0.1 reshape.143
  25.2 0.8 reduce.7
  26.0 0.4 fusion.34
  26.4 0.1 copy.115
  26.5 0.1 copy.118
  26.7 0.8 reshape.144
  27.4 3.4 %all-to-all-start.1 = ((f32[16,1,512]{2,1,0:T(1,128)}), f32[16,1,512]{2,1,0:T(1,128)S(1)}, u32[]{:S(2)}, u32[]{:S(2)}) async-start(f32[16,1,512]{2,1,0:T(1,128)} %reshape.144), calls=%async_computation.1 | async-start | bytes 65536 | tf_op jit(solution)/shard_map/all_to_all | solution.py:19
  31.0 7.1 %all-to-all-done.1 = f32[16,1,512]{2,1,0:T(1,128)S(1)} async-done(((f32[16,1,512]{2,1,0:T(1,128)}), f32[16,1,512]{2,1,0:T(1,128)S(1)}, u32[]{:S(2)}, u32[]{:S(2)}) %all-to-all-start.1) | async-done | bytes 32800 | tf_op jit(solution)/shard_map/all_to_all | solution.py:19
  38.1 0.5 broadcast.46
  38.6 0.7 reduce.12
  39.3 0.1 reshape.145
  39.5 0.3 fusion.8
  39.8 0.3 fusion.4
  40.1 0.1 constant_dynamic-slice_fusion.2
  40.2 0.1 copy.139
  40.3 0.1 copy.140
  40.4 0.1 copy.122
  40.5 0.2 fusion.18
  40.7 0.1 copy.123
  40.8 0.1 copy.127
  40.8 0.1 copy.124
  40.9 0.6 dynamic_update_slice.12
  41.6 0.3 copy.128
  41.8 0.2 fusion.2
  42.1 0.1 dynamic_update_slice.13
  42.1 0.2 maximum_bitcast_fusion
  42.4 19.6 %all_to_all.20 = f32[16,16,2,129]{3,1,2,0:T(8,128)S(1)} all-to-all(f32[16,16,2,129]{3,1,2,0:T(8,128)S(1)} %maximum_bitcast_fusion), channel_id=1, replica_groups=mesh['dp'=32,'mp'=16] {'mp'}, dimensions={0} | all-to-all | bytes 528384 | tf_op jit(solution)/shard_map/all_to_all | solution.py:40
  62.0 0.1 slice_reduce_fusion
  62.1 2.9 %convolution_bitcast_fusion = f32[16,1,8192]{2,0,1:T(8,128)S(1)} fusion(bf16[256,8192]{1,0:T(8,128)(2,1)} %param.22, f32[16,2]{0,1:T(2,128)S(1)} %slice_reduce_fusion, f32[16,2,129]{2,0,1:T(8,128)S(1)} %reduce_sum.52), kind=kOutput, calls=%fused_computation | convolution fusion | flops 67117056 | bytes 4736000 | tf_op jit(solution)/shard_map/dot_general | solution.py:166
  65.0 1.3 %copy.130 = f32[16,1,8192]{2,1,0:T(1,128)} copy(f32[16,1,8192]{2,0,1:T(8,128)S(1)} %convolution_bitcast_fusion) | data formatting | bytes 1048576 | tf_op jit(solution)/shard_map/reshape | solution.py:35
  66.3 3.5 %all-to-all-start.3 = ((f32[16,1,8192]{2,1,0:T(1,128)}), f32[16,1,8192]{2,1,0:T(1,128)S(1)}, u32[]{:S(2)}, u32[]{:S(2)}) async-start(f32[16,1,8192]{2,1,0:T(1,128)} %copy.130), calls=%async_computation.3 | async-start | bytes 1048576 | tf_op jit(solution)/shard_map/all_to_all | solution.py:40
  69.8 16.6 %all-to-all-done.3 = f32[16,1,8192]{2,1,0:T(1,128)S(1)} async-done(((f32[16,1,8192]{2,1,0:T(1,128)}), f32[16,1,8192]{2,1,0:T(1,128)S(1)}, u32[]{:S(2)}, u32[]{:S(2)}) %all-to-all-start.3) | async-done | bytes 524320 | tf_op jit(solution)/shard_map/all_to_all | solution.py:40
  86.4 0.3 reduce_sum.53
  86.8 0.7 multiply_reduce_fusion
  88.2 0.7 multiply_convert_fusion
  (28 shorter events, 0.4 us)
Async XLA Ops:
  0.6 19.1 %copy-start = (bf16[1,1024]{1,0:T(2,128)(2,1)S(1)}, bf16[1,1024]{1,0:T(2,128)(2,1)}, u32[]{:S(2)}) copy-start(bf16[1,1024]{1,0:T(2,128)(2,1)} %param.13) | copy-start | bytes 6148
  0.6 30.2 %copy-start.1 = (bf16[128,1024]{1,0:T(8,128)(2,1)S(1)}, bf16[128,1024]{1,0:T(8,128)(2,1)}, u32[]{:S(2)}) copy-start(bf16[128,1024]{1,0:T(8,128)(2,1)} %param.16) | copy-start | bytes 786436
  0.7 30.2 %copy-start.3 = (bf16[1,64,1024]{2,1,0:T(8,128)(2,1)S(1)}, bf16[1,64,1024]{2,1,0:T(8,128)(2,1)}, u32[]{:S(2)}) copy-start(bf16[1,64,1024]{2,1,0:T(8,128)(2,1)} %param.18) | copy-start | bytes 393220
  0.7 30.3 %copy-start.5 = (bf16[1,1024]{1,0:T(2,128)(2,1)S(1)}, bf16[1,1024]{1,0:T(2,128)(2,1)}, u32[]{:S(2)}) copy-start(bf16[1,1024]{1,0:T(2,128)(2,1)} %param.14) | copy-start | bytes 6148
  4.3 20.7 %all-to-all-start = ((bf16[16,2,2048]{2,1,0:T(2,128)(2,1)}), bf16[16,2,2048]{2,1,0:T(2,128)(2,1)S(1)}, u32[]{:S(2)}, u32[]{:S(2)}) async-start(bf16[16,2,2048]{2,1,0:T(2,128)(2,1)} %reshape.142), calls=%async_computation | async-start | bytes 262144 | tf_op jit(solution)/shard_map/all_to_all | solution.py:19
  27.4 10.6 %all-to-all-start.1 = ((f32[16,1,512]{2,1,0:T(1,128)}), f32[16,1,512]{2,1,0:T(1,128)S(1)}, u32[]{:S(2)}, u32[]{:S(2)}) async-start(f32[16,1,512]{2,1,0:T(1,128)} %reshape.144), calls=%async_computation.1 | async-start | bytes 65536 | tf_op jit(solution)/shard_map/all_to_all | solution.py:19
  42.3 27.5 %copy-start.4 = (bf16[8192]{0:T(1024)(128)(2,1)S(1)}, bf16[8192]{0:T(1024)(128)(2,1)}, u32[]{:S(2)}) copy-start(bf16[8192]{0:T(1024)(128)(2,1)} %param.23) | copy-start | bytes 49156
  62.0 24.8 %copy-start.2 = (bf16[1,8192]{1,0:T(2,128)(2,1)S(1)}, bf16[1,8192]{1,0:T(2,128)(2,1)}, u32[]{:S(2)}) copy-start(bf16[1,8192]{1,0:T(2,128)(2,1)} %param.21) | copy-start | bytes 49156
  66.3 20.1 %all-to-all-start.3 = ((f32[16,1,8192]{2,1,0:T(1,128)}), f32[16,1,8192]{2,1,0:T(1,128)S(1)}, u32[]{:S(2)}, u32[]{:S(2)}) async-start(f32[16,1,8192]{2,1,0:T(1,128)} %copy.130), calls=%async_computation.3 | async-start | bytes 1048576 | tf_op jit(solution)/shard_map/all_to_all | solution.py:40
where the time goes:
time: 89.4 us; the launch traced here: 88.9 us
  waiting for transfers between devices  28.8 us (32%)
  blocking collectives  19.6 us (22%)
  starting transfers between devices  18.7 us (21%)
  local copies, waits for them, and re-layouts  8.51 us (10%)
  other arithmetic  6.23 us (7%)
  matrix products  4.14 us (5%)
  between operations  2.89 us (3%)
    all_to_all x1, blocking collectives, sent_and_summed(): lax.all_to_all(blocks, axis, split_axis=0, concat_axis=0, tiled=True)  19.6 us
    all_to_all x1, waiting for transfers between devices, sent_and_summed(): lax.all_to_all(blocks, axis, split_axis=0, concat_axis=0, tiled=True)  16.6 us
    all_to_all x2, starting transfers between devices, from_everyone(): lax.all_to_all(jnp.broadcast_to(value[None], (length, *value.shape)), axi...  15.2 us
    all_to_all x2, waiting for transfers between devices, from_everyone(): lax.all_to_all(jnp.broadcast_to(value[None], (length, *value.shape)), axi...  12.2 us
    unnamed x23, local copies, waits for them, and re-layouts  3.96 us
    all_to_all x1, starting transfers between devices, sent_and_summed(): lax.all_to_all(blocks, axis, split_axis=0, concat_axis=0, tiled=True)  3.47 us
    dot_general x1, matrix products, local(): jnp.dot(attn, out_weight, preferred_element_type=jnp.float32)  2.89 us
  transfers between devices with their start and end apart: 3, of which 3 were waited for; matrix products, arithmetic and copies ran while one was open for 3% of the time, Pallas kernels for 0%

commit v1 on v0

v1 whole, which is shorter than its diff:
```python
import functools

import jax
import jax.numpy as jnp
from jax import lax
from jax.experimental import pallas as pl
from jax.experimental.pallas import tpu as pltpu
from jax.sharding import PartitionSpec as P

HEAD = 128
KVH = 8
HQ = 32
D = 8192
CHIPS = 8
N = 16
HALF_HEADS = 16
HALF_KV = 4
PRE_DEV = 128
SUF = 64
BLOCK = 256
HALF_COLS = HALF_KV * HEAD
HALF_D = D // 2
GROUPS = 2
GROUP_COLS = HALF_D // GROUPS
NEG = -1e30
F32 = jnp.float32
BF16 = jnp.bfloat16
ORDER = (4, 3, 5, 2, 6, 1, 7)


def nt(a, b):
    return lax.dot_general(a, b, (((1,), (1,)), ((), ())), preferred_element_type=F32)


def nn(a, b):
    return lax.dot_general(a, b, (((1,), (0,)), ((), ())), preferred_element_type=F32)


def kernel(
    q_hbm,
    kn_hbm,
    vn_hbm,
    pk_hbm,
    pv_hbm,
    sk_hbm,
    sv_hbm,
    plen_ref,
    slen_ref,
    res_hbm,
    w_hbm,
    gain_hbm,
    hid_ref,
    nrm_ref,
    qv,
    knv,
    vnv,
    resv,
    gainv,
    kfull,
    vfull,
    kpar,
    vpar,
    bias,
    bpar,
    q32,
    qsend,
    qbuf,
    perm,
    ostage,
    sstage,
    obuf,
    sbuf,
    abuf,
    wbuf,
    ysend,
    rbuf,
    res64,
    gain64,
    loc_sem,
    qs_sem,
    qr_sem,
    xs_sem,
    xr_sem,
    os_sem,
    or_sem,
    ss_sem,
    sr_sem,
    ys_sem,
    yr_sem,
):
    me = lax.axis_index("mp")
    z = me // 2
    c = me % 2
    p = 1 - c
    partner = z * 2 + p

    def at_mp(index):
        return {"mp": index}

    def remote(src, dst, ssem, rsem, index):
        return pltpu.make_async_remote_copy(
            src_ref=src,
            dst_ref=dst,
            send_sem=ssem,
            recv_sem=rsem,
            device_id=at_mp(index),
            device_id_type=pl.DeviceIdType.MESH,
        )

    barrier = pltpu.get_barrier_semaphore()
    for step in range(1, N):
        pl.semaphore_signal(
            barrier,
            inc=1,
            device_id=at_mp((me + step) % N),
            device_id_type=pl.DeviceIdType.MESH,
        )

    own_cols = pl.ds(pl.multiple_of(c * HALF_COLS, HALF_COLS), HALF_COLS)
    par_cols = pl.ds(pl.multiple_of(p * HALF_COLS, HALF_COLS), HALF_COLS)
    own_d = pl.ds(pl.multiple_of(c * HALF_D, HALF_D), HALF_D)
    par_d = pl.ds(pl.multiple_of(p * HALF_D, HALF_D), HALF_D)

    local = [
        pltpu.make_async_copy(q_hbm, qv, loc_sem.at[0]),
        pltpu.make_async_copy(kn_hbm, knv, loc_sem.at[1]),
        pltpu.make_async_copy(vn_hbm, vnv, loc_sem.at[2]),
        pltpu.make_async_copy(pk_hbm, kfull.at[pl.ds(0, PRE_DEV)], loc_sem.at[3]),
        pltpu.make_async_copy(pv_hbm, vfull.at[pl.ds(0, PRE_DEV)], loc_sem.at[4]),
        pltpu.make_async_copy(sk_hbm.at[0], kfull.at[pl.ds(PRE_DEV, SUF)], loc_sem.at[5]),
        pltpu.make_async_copy(sv_hbm.at[0], vfull.at[pl.ds(PRE_DEV, SUF)], loc_sem.at[6]),
        pltpu.make_async_copy(res_hbm, resv, loc_sem.at[7]),
        pltpu.make_async_copy(gain_hbm, gainv, loc_sem.at[8]),
        pltpu.make_async_copy(w_hbm.at[:, own_d], wbuf.at[c], loc_sem.at[9]),
    ]
    for copy in local:
        copy.start()

    rows = lax.broadcasted_iota(jnp.int32, (BLOCK, BLOCK), 0)
    cols = lax.broadcasted_iota(jnp.int32, (BLOCK, BLOCK), 1)
    perm[...] = jnp.where(cols == (rows % N) * N + rows // N, 1.0, 0.0).astype(BF16)
    col = lax.broadcasted_iota(jnp.int32, (8, BLOCK), 1)
    valid = (
        ((col < PRE_DEV) & (col + me * PRE_DEV < plen_ref[0]))
        | ((col >= PRE_DEV) & (col < PRE_DEV + SUF) & (col - PRE_DEV < slen_ref[0]))
        | (col == PRE_DEV + SUF)
    )
    bias[...] = jnp.where(valid, 0.0, NEG)

    local[0].wait()
    for h in range(HQ):
        q32[h : h + 1, :] = qv[0:1, h * HEAD : (h + 1) * HEAD].astype(F32)
    qsend[0] = q32[0:HALF_HEADS, :].astype(BF16)
    qsend[1] = q32[HALF_HEADS:HQ, :].astype(BF16)
    qbuf[me] = qsend[c]

    pad_rows = BLOCK - PRE_DEV - SUF
    first = lax.broadcasted_iota(jnp.int32, (pad_rows, KVH * HEAD), 0) == 0
    local[1].wait()
    kfull[PRE_DEV + SUF : BLOCK, :] = jnp.where(first, knv[0:1, :].astype(F32), 0.0).astype(BF16)
    local[2].wait()
    vfull[PRE_DEV + SUF : BLOCK, :] = jnp.where(first, vnv[0:1, :].astype(F32), 0.0).astype(BF16)

    pl.semaphore_wait(barrier, N - 1)

    sends = []
    for step in ORDER:
        for half in range(2):
            target = ((z + step) % CHIPS) * 2 + half
            copy = remote(
                qsend.at[half], qbuf.at[me], qs_sem.at[step * 2 + half], qr_sem.at[me], target
            )
            copy.start()
            sends.append(copy)
    copy = remote(qsend.at[p], qbuf.at[me], qs_sem.at[0], qr_sem.at[me], partner)
    copy.start()
    sends.append(copy)

    for copy in local[3:7]:
        copy.wait()
    swaps = [
        remote(kfull.at[:, par_cols], kpar, xs_sem.at[0], xr_sem.at[0], partner),
        remote(vfull.at[:, par_cols], vpar, xs_sem.at[1], xr_sem.at[1], partner),
        remote(bias, bpar, xs_sem.at[2], xr_sem.at[2], partner),
        remote(w_hbm.at[:, par_d], wbuf.at[c], xs_sem.at[3], xr_sem.at[3], partner),
    ]
    for copy in swaps:
        copy.start()

    local[7].wait()
    local[8].wait()
    for r in range(D // HEAD):
        res64[r : r + 1, :] = resv[0:1, r * HEAD : (r + 1) * HEAD].astype(F32)
        gain64[r : r + 1, :] = gainv[0:1, r * HEAD : (r + 1) * HEAD].astype(F32)

    for copy in swaps[0:3]:
        copy.wait_recv()
    for step in range(1, N):
        source = (me + step) % N
        remote(qsend.at[0], qbuf.at[source], qs_sem.at[0], qr_sem.at[source], source).wait_recv()

    queries = nn(perm[...], qbuf[...].reshape(N * HALF_HEADS, HEAD)).astype(BF16)
    row64 = lax.broadcasted_iota(jnp.int32, (64, BLOCK), 0) % N
    col64 = lax.broadcasted_iota(jnp.int32, (64, BLOCK), 1)
    shown_own = (col64 < PRE_DEV) | (row64 == me)
    shown_par = (col64 < PRE_DEV) | (row64 == partner)
    lane16 = lax.broadcasted_iota(jnp.int32, (N, HEAD), 1) % N
    sub16 = lax.broadcasted_iota(jnp.int32, (N, HEAD), 0)
    diagonal = lane16 == sub16
    scale = HEAD ** (-0.5)
    bias_own = bias[0:1, :]
    bias_par = bpar[0:1, :]
    for j in range(HALF_KV):
        qj = queries[64 * j : 64 * (j + 1), :]
        own_j = pl.ds(pl.multiple_of(c * HALF_COLS + j * HEAD, HEAD), HEAD)
        s_own = nt(qj, kfull[:, own_j]) * scale + bias_own
        s_par = nt(qj, kpar[:, j * HEAD : (j + 1) * HEAD]) * scale + bias_par
        s_own = jnp.where(shown_own, s_own, NEG)
        s_par = jnp.where(shown_par, s_par, NEG)
        top = jnp.max(jnp.maximum(s_own, s_par), axis=1, keepdims=True)
        w_own = jnp.exp(s_own - top)
        w_par = jnp.exp(s_par - top)
        total = jnp.sum(w_own + w_par, axis=1, keepdims=True)
        out = nn(w_own.astype(BF16), vfull[:, own_j]) + nn(
            w_par.astype(BF16), vpar[:, j * HEAD : (j + 1) * HEAD]
        )
        for hh in range(4):
            part = slice(N * hh, N * (hh + 1))
            ostage[4 * j + hh] = out[part, :].astype(BF16)
            tops = jnp.sum(jnp.where(diagonal, top[part, :], 0.0), axis=0, keepdims=True)
            totals = jnp.sum(jnp.where(diagonal, total[part, :], 0.0), axis=0, keepdims=True)
            g = 2 * j + hh // 2
            sstage[g, hh % 2 : hh % 2 + 1, :] = tops
            sstage[g, 2 + hh % 2 : 3 + hh % 2, :] = totals
        for d in range(2):
            g = 2 * j + d
            target = (4 * c + j) * 2 + d
            for src, dst, ssem, rsem in (
                (ostage.at[pl.ds(2 * g, 2)], obuf.at[:, z], os_sem.at[g], or_sem.at[z]),
                (sstage.at[g], sbuf.at[z], ss_sem.at[g], sr_sem.at[z]),
            ):

                @pl.when(target != me)
                def _():
                    remote(src, dst, ssem, rsem, target).start()

                @pl.when(target == me)
                def _():
                    pltpu.make_async_copy(src, dst, rsem).start()

    for src_z in range(CHIPS):
        pltpu.make_async_copy(obuf.at[:, src_z], obuf.at[:, src_z], or_sem.at[src_z]).wait()
        pltpu.make_async_copy(sbuf.at[src_z], sbuf.at[src_z], sr_sem.at[src_z]).wait()
    stats = sbuf[...]
    group = lax.broadcasted_iota(jnp.int32, (2, HEAD), 1) // N
    most = stats[0, 0:2, :]
    for src_z in range(1, CHIPS):
        most = jnp.maximum(most, stats[src_z, 0:2, :])
    summed = jnp.zeros((2, HEAD), F32)
    factor = jnp.zeros((2, HEAD), F32)
    for src_z in range(CHIPS):
        f = jnp.exp(stats[src_z, 0:2, :] - most)
        summed = summed + f * stats[src_z, 2:4, :]
        factor = jnp.where(group == src_z, f, factor)
    factor = factor / summed
    for hh in range(2):
        mix = jnp.where(diagonal, factor[hh : hh + 1, :], 0.0)
        high = mix.astype(BF16)
        low = (mix - high.astype(F32)).astype(BF16)
        rows_h = obuf[hh].reshape(CHIPS * N, HEAD)
        abuf[c, :, hh * HEAD : (hh + 1) * HEAD] = (nn(high, rows_h) + nn(low, rows_h)).astype(BF16)
    attn_swap = remote(abuf.at[c], abuf.at[c], xs_sem.at[4], xr_sem.at[4], partner)
    attn_swap.start()

    local[9].wait()
    swaps[3].wait_recv()
    attn_swap.wait_recv()
    for group_at in range(GROUPS):
        at = slice(group_at * GROUP_COLS, (group_at + 1) * GROUP_COLS)
        y = nn(abuf[0], wbuf[0, :, at]) + nn(abuf[1], wbuf[1, :, at])
        y = y.astype(BF16)
        y = jnp.concatenate([y[:, HEAD * i : HEAD * (i + 1)] for i in range(N)], axis=0)
        y = nn(perm[...], y).astype(BF16)
        ysend[group_at] = y.reshape(N, N, HEAD)
        for step in ORDER:
            for half in range(2):
                target = ((z + step) % CHIPS) * 2 + half
                at_sem = group_at * N + step * 2 + half
                copy = remote(
                    ysend.at[group_at, target],
                    rbuf.at[z, c, group_at],
                    ys_sem.at[at_sem],
                    yr_sem.at[z, c, group_at],
                    target,
                )
                copy.start()
                sends.append(copy)
        copy = remote(
            ysend.at[group_at, partner],
            rbuf.at[z, c, group_at],
            ys_sem.at[group_at * N],
            yr_sem.at[z, c, group_at],
            partner,
        )
        copy.start()
        sends.append(copy)
        rbuf[z, c, group_at] = ysend[group_at, me]

    for step in range(1, N):
        source = (me + step) % N
        for group_at in range(GROUPS):
            at = rbuf.at[source // 2, source % 2, group_at]
            pltpu.make_async_copy(at, at, yr_sem.at[source // 2, source % 2, group_at]).wait()
    stream = res64[...] + jnp.sum(rbuf[...].astype(F32), axis=0).reshape(D // HEAD, HEAD)
    meansq = jnp.sum(stream * stream, keepdims=True) * (1.0 / D)
    normed = stream * lax.rsqrt(meansq + 1e-05) * gain64[...]
    hid_ref[...] = stream.astype(BF16)
    nrm_ref[...] = normed.astype(BF16)

    for copy in sends:
        copy.wait_send()
    for copy in swaps:
        copy.wait_send()
    attn_swap.wait_send()
    for j in range(HALF_KV):
        for d in range(2):
            g = 2 * j + d
            target = (4 * c + j) * 2 + d

            @pl.when(target != me)
            def _():
                remote(
                    ostage.at[pl.ds(2 * g, 2)], obuf.at[:, z], os_sem.at[g], or_sem.at[z], target
                ).wait_send()
                remote(
                    sstage.at[g], sbuf.at[z], ss_sem.at[g], sr_sem.at[z], target
                ).wait_send()


def local(
    query_new,
    key_new,
    value_new,
    prefix_keys,
    prefix_values,
    sample_suffix_keys,
    sample_suffix_values,
    prefix_len,
    suffix_len,
    residual,
    out_weight,
    norm_gain,
):
    hbm = pl.BlockSpec(memory_space=pl.ANY)
    smem = pl.BlockSpec(memory_space=pltpu.SMEM)
    vmem = pl.BlockSpec(memory_space=pltpu.VMEM)
    dma = pltpu.SemaphoreType.DMA
    hidden, normed = pl.pallas_call(
        kernel,
        out_shape=(
            jax.ShapeDtypeStruct((D // HEAD, HEAD), BF16),
            jax.ShapeDtypeStruct((D // HEAD, HEAD), BF16),
        ),
        in_specs=[hbm] * 7 + [smem] * 2 + [hbm] * 3,
        out_specs=(vmem, vmem),
        scratch_shapes=[
            pltpu.VMEM((1, HQ * HEAD), BF16),
            pltpu.VMEM((1, KVH * HEAD), BF16),
            pltpu.VMEM((1, KVH * HEAD), BF16),
            pltpu.VMEM((1, D), BF16),
            pltpu.VMEM((1, D), BF16),
            pltpu.VMEM((BLOCK, KVH * HEAD), BF16),
            pltpu.VMEM((BLOCK, KVH * HEAD), BF16),
            pltpu.VMEM((BLOCK, HALF_COLS), BF16),
            pltpu.VMEM((BLOCK, HALF_COLS), BF16),
            pltpu.VMEM((8, BLOCK), F32),
            pltpu.VMEM((8, BLOCK), F32),
            pltpu.VMEM((HQ, HEAD), F32),
            pltpu.VMEM((2, HALF_HEADS, HEAD), BF16),
            pltpu.VMEM((N, HALF_HEADS, HEAD), BF16),
            pltpu.VMEM((BLOCK, BLOCK), BF16),
            pltpu.VMEM((HALF_HEADS, N, HEAD), BF16),
            pltpu.VMEM((CHIPS, 4, HEAD), F32),
            pltpu.VMEM((2, CHIPS, N, HEAD), BF16),
            pltpu.VMEM((CHIPS, 4, HEAD), F32),
            pltpu.VMEM((2, N, 2 * HEAD), BF16),
            pltpu.VMEM((2, 2 * HEAD, HALF_D), BF16),
            pltpu.VMEM((GROUPS, N, N, HEAD), BF16),
            pltpu.VMEM((CHIPS, 2, GROUPS, N, HEAD), BF16),
            pltpu.VMEM((D // HEAD, HEAD), F32),
            pltpu.VMEM((D // HEAD, HEAD), F32),
            dma((10,)),
            dma((N,)),
            dma((N,)),
            dma((5,)),
            dma((5,)),
            dma((CHIPS,)),
            dma((CHIPS,)),
            dma((CHIPS,)),
            dma((CHIPS,)),
            dma((GROUPS * N,)),
            dma((CHIPS, 2, GROUPS)),
        ],
        compiler_params=pltpu.CompilerParams(collective_id=0, has_side_effects=True),
        name="decode_step",
    )(
        query_new,
        key_new,
        value_new,
        prefix_keys,
        prefix_values,
        sample_suffix_keys,
        sample_suffix_values,
        prefix_len,
        suffix_len,
        residual,
        out_weight,
        norm_gain.reshape(1, D),
    )
    return hidden.reshape(1, D), normed.reshape(1, D)


def solution(mesh):
    placed = (
        P(("dp", "mp"), None),
        P(("dp", "mp"), None),
        P(("dp", "mp"), None),
        P(("dp", "mp"), None),
        P(("dp", "mp"), None),
        P(("dp", "mp"), None, None),
        P(("dp", "mp"), None, None),
        P("dp"),
        P(("dp", "mp")),
        P(("dp", "mp"), None),
        P("mp", None),
        P(),
    )
    return jax.shard_map(
        local,
        mesh=mesh,
        in_specs=placed,
        out_specs=(P(("dp", "mp"), None), P(("dp", "mp"), None)),
        check_vma=False,
    )
```

time: 89.4 us -> 36.9 us (0.41)
  Pallas kernels: 0 us -> 31.9 us
  waiting for transfers between devices: 28.8 us -> 0 us
  blocking collectives: 19.6 us -> 0 us
  starting transfers between devices: 18.7 us -> 0 us
  other arithmetic: 6.23 us -> 0 us
  local copies, waits for them, and re-layouts: 8.51 us -> 2.76 us
  matrix products: 4.14 us -> 0 us
  between operations: 2.89 us -> 1.93 us
    pallas_call x0 -> x1, Pallas kernels: none -> 31.9 us  [local(): pl.pallas_call(kernel, out_shape=(jax.ShapeDtypeStruct((D // HEAD, HEAD),...]
    all_to_all x3 -> x0, waiting for transfers between devices: 28.8 us -> none  [the longest x1 16.6 us: sent_and_summed(): lax.all_to_all(blocks, axis, split_axis=0, concat_axis=0, tiled=True)]
    all_to_all x1 -> x0, blocking collectives: 19.6 us -> none  [sent_and_summed(): lax.all_to_all(blocks, axis, split_axis=0, concat_axis=0, tiled=True)]
    all_to_all x3 -> x0, starting transfers between devices: 18.7 us -> none  [the longest x2 15.2 us: from_everyone(): lax.all_to_all(jnp.broadcast_to(value[None], (length, *value.shape)), axi...]
    dot_general x6 -> x0, matrix products: 4.14 us -> none  [the longest x1 2.89 us: local(): jnp.dot(attn, out_weight, preferred_element_type=jnp.float32)]
    unnamed x23 -> x0, local copies, waits for them, and re-layouts: 3.96 us -> none
    reduce_sum x5 -> x0, other arithmetic: 1.52 us -> none  [the longest x1 0.67 us: local(): meansq = jnp.mean(stream * stream, axis=-1, keepdims=True)]
    all_to_all x2 -> x0, other arithmetic: 1.49 us -> none  [from_everyone(): lax.all_to_all(jnp.broadcast_to(value[None], (length, *value.shape)), axi...]
  transfers between devices with their start and end apart: 3 -> 0, of which waited for: 3 -> 0; matrix products, arithmetic and copies ran while one was open for 3% -> 0% of each run, Pallas kernels for 0% -> 0%
where the time goes in v1:
time: 36.9 us; the launch traced here: 36.5 us
  Pallas kernels  31.9 us (86%)
  local copies, waits for them, and re-layouts  2.76 us (7%)
  between operations  1.93 us (5%)
    pallas_call x1, Pallas kernels, local(): pl.pallas_call(kernel, out_shape=(jax.ShapeDtypeStruct((D // HEAD, HEAD),...  31.9 us
    reshape x1, local copies, waits for them, and re-layouts, local(): return (hidden.reshape(1, D), normed.reshape(1, D))  1.41 us
    reshape x1, local copies, waits for them, and re-layouts, local(): norm_gain.reshape(1, D)  1.35 us

profile of v1, /device:TPU:1, one launch (start us, length us, event | category | flops | bytes accessed | tf_op | source)
XLA Modules:
  0.0 36.5 jit_solution(8977379819495436914)
XLA Ops:
  1.9 1.4 %reshape.13.gain_hbm = bf16[1,8192]{1,0:T(2,128)(2,1)} reshape(bf16[8192]{0:T(1024)(128)(2,1)} %param.23) | data formatting | bytes 32768 | tf_op jit(solution)/shard_map/reshape | solution.py:418
  3.3 31.9 %decode_step.1 = (bf16[64,128]{1,0:T(8,128)(2,1)}, bf16[64,128]{1,0:T(8,128)(2,1)}) custom-call(bf16[1,4096]{1,0:T(2,128)(2,1)} %q_hbm.1, bf16[1,1024]{1,0:T(2,128)(2,1)} %kn_hbm.1, bf16[1,1024]{1,0:T(2,128)(2,1)} %vn_hbm.1, bf16[128,1024]{1,0:T(8,128)(2,1)} %pk_hbm.1, bf16[128,1024]{1,0:T(8,128)(2,1)} %pv_hbm.1, bf16[1,64,1024]{2,1,0:T(8,128)(2,1)} %sk_hbm.1, ...), custom_call_target="tpu_custom_call" | custom-call | tf_op jit(solution)/shard_map/decode_step/pallas_call | solution.py:358
  35.1 1.4 %copy_bitcast_fusion = (bf16[1,8192]{1,0:T(2,128)(2,1)}, bf16[1,8192]{1,0:T(2,128)(2,1)}) fusion(bf16[1,1,64,128]{3,2,1,0:T(8,128)(2,1)} %bitcast.9, bf16[1,1,64,128]{3,2,1,0:T(8,128)(2,1)} %bitcast.8), kind=kLoop, calls=%fused_computation | loop fusion | bytes 65536 | tf_op jit(solution)/shard_map/reshape | solution.py:420

commit v2 on v1

v2 whole, which is shorter than its diff:
```python
import functools

import jax
import jax.numpy as jnp
from jax import lax
from jax.experimental import pallas as pl
from jax.experimental.pallas import tpu as pltpu
from jax.sharding import PartitionSpec as P

HEAD = 128
KVH = 8
HQ = 32
D = 8192
CHIPS = 8
N = 16
HALF_HEADS = 16
HALF_KV = 4
PRE_DEV = 128
SUF = 64
BLOCK = 256
HALF_COLS = HALF_KV * HEAD
HALF_D = D // 2
GROUPS = 2
GROUP_COLS = HALF_D // GROUPS
NEG = -1e30
F32 = jnp.float32
BF16 = jnp.bfloat16
HALF_CHIPS = CHIPS // 2
SB = N // 2
RB = 4 * SB


def nt(a, b):
    return lax.dot_general(a, b, (((1,), (1,)), ((), ())), preferred_element_type=F32)


def nn(a, b):
    return lax.dot_general(a, b, (((1,), (0,)), ((), ())), preferred_element_type=F32)


def kernel(
    q_hbm,
    kn_hbm,
    vn_hbm,
    pk_hbm,
    pv_hbm,
    sk_hbm,
    sv_hbm,
    plen_hbm,
    slen_hbm,
    res_hbm,
    w_hbm,
    gain_hbm,
    hid_ref,
    nrm_ref,
    qv,
    knv,
    vnv,
    resv,
    gainv,
    kfull,
    vfull,
    kpar,
    vpar,
    bias,
    bpar,
    q32,
    qsend,
    qbuf,
    to_heads,
    to_samples,
    ostage,
    sstage,
    obuf,
    sbuf,
    wbuf,
    ysend,
    rbuf,
    res64,
    gain64,
    plen_ref,
    slen_ref,
    loc_sem,
    qs_sem,
    qr_sem,
    xs_sem,
    xr_sem,
    os_sem,
    or_sem,
    ss_sem,
    sr_sem,
    ys_sem,
    yr_sem,
):
    me = lax.axis_index("mp")
    z = me // 2
    c = me % 2
    p = 1 - c
    partner = z * 2 + p
    my_batch = z // HALF_CHIPS

    def at_mp(index):
        return {"mp": index}

    def remote(src, dst, ssem, rsem, index):
        return pltpu.make_async_remote_copy(
            src_ref=src,
            dst_ref=dst,
            send_sem=ssem,
            recv_sem=rsem,
            device_id=at_mp(index),
            device_id_type=pl.DeviceIdType.MESH,
        )

    def wait_bytes(ref, sem):
        pltpu.make_async_copy(ref, ref, sem).wait()

    own_cols = pl.ds(pl.multiple_of(c * HALF_COLS, HALF_COLS), HALF_COLS)
    par_cols = pl.ds(pl.multiple_of(p * HALF_COLS, HALF_COLS), HALF_COLS)
    own_d = pl.ds(pl.multiple_of(c * HALF_D, HALF_D), HALF_D)
    par_d = pl.ds(pl.multiple_of(p * HALF_D, HALF_D), HALF_D)
    swaps = [
        remote(kfull.at[:, par_cols], kpar, xs_sem.at[0], xr_sem.at[0], partner),
        remote(vfull.at[:, par_cols], vpar, xs_sem.at[1], xr_sem.at[1], partner),
        remote(bias, bpar, xs_sem.at[2], xr_sem.at[2], partner),
        remote(w_hbm.at[:, par_d], wbuf.at[c], xs_sem.at[3], xr_sem.at[3], partner),
    ]
    local = [
        pltpu.make_async_copy(q_hbm, qv, loc_sem.at[0]),
        pltpu.make_async_copy(kn_hbm, knv, loc_sem.at[1]),
        pltpu.make_async_copy(vn_hbm, vnv, loc_sem.at[2]),
        pltpu.make_async_copy(pk_hbm, kfull.at[pl.ds(0, PRE_DEV)], loc_sem.at[3]),
        pltpu.make_async_copy(pv_hbm, vfull.at[pl.ds(0, PRE_DEV)], loc_sem.at[4]),
        pltpu.make_async_copy(sk_hbm.at[0], kfull.at[pl.ds(PRE_DEV, SUF)], loc_sem.at[5]),
        pltpu.make_async_copy(sv_hbm.at[0], vfull.at[pl.ds(PRE_DEV, SUF)], loc_sem.at[6]),
        pltpu.make_async_copy(res_hbm, resv, loc_sem.at[7]),
        pltpu.make_async_copy(gain_hbm, gainv, loc_sem.at[8]),
        pltpu.make_async_copy(w_hbm.at[:, own_d], wbuf.at[c], loc_sem.at[9]),
        pltpu.make_async_copy(plen_hbm, plen_ref, loc_sem.at[10]),
        pltpu.make_async_copy(slen_hbm, slen_ref, loc_sem.at[11]),
    ]

    with jax.named_scope("prep"):
        barrier = pltpu.get_barrier_semaphore()

        def greet(step, carry):
            pl.semaphore_signal(
                barrier,
                inc=1,
                device_id=at_mp((me + step) % N),
                device_id_type=pl.DeviceIdType.MESH,
            )
            return carry

        lax.fori_loop(1, N, greet, 0)
        for copy in local:
            copy.start()

        rows = lax.broadcasted_iota(jnp.int32, (HEAD, HEAD), 0)
        cols = lax.broadcasted_iota(jnp.int32, (HEAD, HEAD), 1)
        to_heads[...] = jnp.where(cols == (rows % SB) * N + rows // SB, 1.0, 0.0).astype(BF16)
        to_samples[...] = jnp.where(cols == (rows % N) * SB + rows // N, 1.0, 0.0).astype(BF16)
        local[10].wait()
        local[11].wait()
        col = lax.broadcasted_iota(jnp.int32, (8, BLOCK), 1)
        valid = (
            ((col < PRE_DEV) & (col + me * PRE_DEV < plen_ref[0]))
            | ((col >= PRE_DEV) & (col < PRE_DEV + SUF) & (col - PRE_DEV < slen_ref[0]))
            | (col == PRE_DEV + SUF)
        )
        bias[...] = jnp.where(valid, 0.0, NEG)

        local[0].wait()
        for h in range(HQ):
            q32[h : h + 1, :] = qv[0:1, h * HEAD : (h + 1) * HEAD].astype(F32)
        qsend[0] = q32[0:HALF_HEADS, :].astype(BF16)
        qsend[1] = q32[HALF_HEADS:HQ, :].astype(BF16)

        pad_rows = BLOCK - PRE_DEV - SUF
        first = lax.broadcasted_iota(jnp.int32, (pad_rows, KVH * HEAD), 0) == 0
        local[1].wait()
        kfull[PRE_DEV + SUF : BLOCK, :] = jnp.where(first, knv[0:1, :].astype(F32), 0.0).astype(
            BF16
        )
        local[2].wait()
        vfull[PRE_DEV + SUF : BLOCK, :] = jnp.where(first, vnv[0:1, :].astype(F32), 0.0).astype(
            BF16
        )

    with jax.named_scope("barrier"):
        pl.semaphore_wait(barrier, N - 1)

    with jax.named_scope("qsend"):

        def send_query(i, carry):
            k = i // 2
            half = i % 2
            step = CHIPS // 2 + ((k + 1) // 2) * (1 - 2 * (k % 2))
            target = ((z + step) % CHIPS) * 2 + half
            remote(qsend.at[half], qbuf.at[me], qs_sem, qr_sem.at[my_batch], target).start()
            return carry

        lax.fori_loop(0, N - 2, send_query, 0)
        remote(qsend.at[p], qbuf.at[me], qs_sem, qr_sem.at[my_batch], partner).start()
        pltpu.make_async_copy(qsend.at[c], qbuf.at[me], qr_sem.at[my_batch]).start()

    with jax.named_scope("kvsend"):
        for copy in local[3:7]:
            copy.wait()
        for copy in swaps:
            copy.start()

    with jax.named_scope("resgain"):
        local[7].wait()
        local[8].wait()
        for r in range(D // HEAD):
            res64[r : r + 1, :] = resv[0:1, r * HEAD : (r + 1) * HEAD].astype(F32)
            gain64[r, :] = gainv[r * HEAD : (r + 1) * HEAD].astype(F32)

    with jax.named_scope("kvwait"):
        for copy in swaps[0:3]:
            copy.wait_recv()

    scale = HEAD ** (-0.5)
    row32 = lax.broadcasted_iota(jnp.int32, (RB, BLOCK), 0)
    col32 = lax.broadcasted_iota(jnp.int32, (RB, BLOCK), 1)
    diagonal = col32 % RB == row32

    def attend(b):
        with jax.named_scope("qwait%d" % b):
            wait_bytes(qbuf.at[pl.ds(SB * b, SB)], qr_sem.at[b])
        with jax.named_scope("attn%d" % b):
            queries = nn(
                to_heads[...], qbuf[SB * b : SB * (b + 1)].reshape(SB * HALF_HEADS, HEAD)
            ).astype(BF16)
            shown_own = (col32 < PRE_DEV) | (row32 % SB + SB * b == me)
            shown_par = (col32 < PRE_DEV) | (row32 % SB + SB * b == partner)
            bias_own = jnp.where(shown_own, bias[0:1, :], NEG)
            bias_par = jnp.where(shown_par, bpar[0:1, :], NEG)
            for j in range(HALF_KV):
                qj = queries[RB * j : RB * (j + 1), :]
                own_j = pl.ds(pl.multiple_of(c * HALF_COLS + j * HEAD, HEAD), HEAD)
                s_own = nt(qj, kfull[:, own_j]) * scale + bias_own
                s_par = nt(qj, kpar[:, j * HEAD : (j + 1) * HEAD]) * scale + bias_par
                top = jnp.max(jnp.maximum(s_own, s_par), axis=1, keepdims=True)
                w_own = jnp.exp(s_own - top)
                w_par = jnp.exp(s_par - top)
                total = jnp.sum(w_own + w_par, axis=1, keepdims=True)
                out = nn(w_own.astype(BF16), vfull[:, own_j]) + nn(
                    w_par.astype(BF16), vpar[:, j * HEAD : (j + 1) * HEAD]
                )
                ostage[b, j] = out.astype(BF16)
                sstage[b, j, 0:1, :] = jnp.sum(
                    jnp.where(diagonal, top, 0.0), axis=0, keepdims=True
                )
                sstage[b, j, 1:2, :] = jnp.sum(
                    jnp.where(diagonal, total, 0.0), axis=0, keepdims=True
                )
        with jax.named_scope("osend%d" % b):
            for i in (1, 2, 3, 0):
                j = (z + i) % HALF_CHIPS
                for half in range(2):
                    target = (HALF_CHIPS * c + j) * 2 + half
                    pairs = (
                        (ostage.at[b, j], obuf.at[b, z], os_sem.at[b], or_sem.at[b]),
                        (sstage.at[b, j], sbuf.at[b, z], ss_sem.at[b], sr_sem.at[b]),
                    )
                    if i:
                        for src, dst, ssem, rsem in pairs:
                            remote(src, dst, ssem, rsem, target).start()
                        continue

                    @pl.when(target != me)
                    def _():
                        for src, dst, ssem, rsem in pairs:
                            remote(src, dst, ssem, rsem, target).start()

                    @pl.when(target == me)
                    def _():
                        for src, dst, ssem, rsem in pairs:
                            pltpu.make_async_copy(src, dst, rsem).start()

    def project(b):
        with jax.named_scope("owait%d" % b):
            wait_bytes(obuf.at[b], or_sem.at[b])
            wait_bytes(sbuf.at[b], sr_sem.at[b])
        with jax.named_scope("combine%d" % b):
            stats = sbuf[b]
            group = lax.broadcasted_iota(jnp.int32, (1, BLOCK), 1) // RB
            most = stats[0, 0:1, :]
            for src_z in range(1, CHIPS):
                most = jnp.maximum(most, stats[src_z, 0:1, :])
            summed = jnp.zeros((1, BLOCK), F32)
            factor = jnp.zeros((1, BLOCK), F32)
            for src_z in range(CHIPS):
                f = jnp.exp(stats[src_z, 0:1, :] - most)
                summed = summed + f * stats[src_z, 1:2, :]
                factor = jnp.where(group == src_z, f, factor)
            mix = jnp.where(diagonal, factor / summed, 0.0)
            high = mix.astype(BF16)
            low = (mix - high.astype(F32)).astype(BF16)
            parts = obuf[b].reshape(CHIPS * RB, HEAD)
            attn = nn(high, parts) + nn(low, parts)
            attn = jnp.concatenate([attn[SB * h : SB * (h + 1), :] for h in range(4)], axis=1)
            attn = attn.astype(BF16)
        if b == 0:
            with jax.named_scope("waitw"):
                local[9].wait()
                swaps[3].wait_recv()
        for g in range(GROUPS):
            with jax.named_scope("proj%d%d" % (b, g)):
                at = slice(g * GROUP_COLS, (g + 1) * GROUP_COLS)
                y = nn(attn[:, 0 : 2 * HEAD], wbuf[0, :, at]) + nn(
                    attn[:, 2 * HEAD : 4 * HEAD], wbuf[1, :, at]
                )
                y = jnp.concatenate([y[:, HEAD * i : HEAD * (i + 1)] for i in range(N)], axis=0)
                y = nn(to_samples[...], y.astype(BF16)).astype(BF16)
                ysend[b, g] = y.reshape(SB, N, HEAD)
            with jax.named_scope("ysend%d%d" % (b, g)):

                def send_projection(t, carry):
                    target = SB * b + t

                    @pl.when(target != me)
                    def _():
                        remote(
                            ysend.at[b, g, t], rbuf.at[z, c, g], ys_sem.at[b, g], yr_sem, target
                        ).start()

                    @pl.when(target == me)
                    def _():
                        pltpu.make_async_copy(
                            ysend.at[b, g, t], rbuf.at[z, c, g], yr_sem
                        ).start()

                    return carry

                lax.fori_loop(0, SB, send_projection, 0)

    attend(0)
    attend(1)
    project(0)
    project(1)

    with jax.named_scope("sendwait"):
        wait_bytes(qbuf.at[pl.ds(0, N - 1)], qs_sem)
        for copy in swaps:
            copy.wait_send()

        for b in range(2):
            own_chip = z // HALF_CHIPS == c

            @pl.when(own_chip)
            def _():
                wait_bytes(obuf.at[b, pl.ds(0, CHIPS - 1)], os_sem.at[b])
                wait_bytes(sbuf.at[b, pl.ds(0, CHIPS - 1)], ss_sem.at[b])

            @pl.when(jnp.logical_not(own_chip))
            def _():
                wait_bytes(obuf.at[b], os_sem.at[b])
                wait_bytes(sbuf.at[b], ss_sem.at[b])

    with jax.named_scope("ywait"):
        wait_bytes(rbuf, yr_sem)
    with jax.named_scope("final"):
        stream = res64[...] + jnp.sum(rbuf[...].astype(F32), axis=0).reshape(D // HEAD, HEAD)
        meansq = jnp.sum(stream * stream, keepdims=True) * (1.0 / D)
        normed = stream * lax.rsqrt(meansq + 1e-05) * gain64[...]
        hid_ref[...] = stream.astype(BF16)
        nrm_ref[...] = normed.astype(BF16)
    with jax.named_scope("sendwait2"):
        for b in range(2):
            for g in range(GROUPS):

                @pl.when(my_batch == b)
                def _():
                    wait_bytes(ysend.at[b, g, pl.ds(0, SB - 1)], ys_sem.at[b, g])

                @pl.when(my_batch != b)
                def _():
                    wait_bytes(ysend.at[b, g], ys_sem.at[b, g])


def local(
    query_new,
    key_new,
    value_new,
    prefix_keys,
    prefix_values,
    sample_suffix_keys,
    sample_suffix_values,
    prefix_len,
    suffix_len,
    residual,
    out_weight,
    norm_gain,
):
    hbm = pl.BlockSpec(memory_space=pl.ANY)
    vmem = pl.BlockSpec(memory_space=pltpu.VMEM)
    dma = pltpu.SemaphoreType.DMA
    hidden, normed = pl.pallas_call(
        kernel,
        out_shape=(
            pltpu.VMEM((D // HEAD, HEAD), BF16),
            pltpu.VMEM((D // HEAD, HEAD), BF16),
        ),
        in_specs=[hbm] * 12,
        out_specs=(vmem, vmem),
        scratch_shapes=[
            pltpu.VMEM((1, HQ * HEAD), BF16),
            pltpu.VMEM((1, KVH * HEAD), BF16),
            pltpu.VMEM((1, KVH * HEAD), BF16),
            pltpu.VMEM((1, D), BF16),
            pltpu.VMEM((D,), BF16),
            pltpu.VMEM((BLOCK, KVH * HEAD), BF16),
            pltpu.VMEM((BLOCK, KVH * HEAD), BF16),
            pltpu.VMEM((BLOCK, HALF_COLS), BF16),
            pltpu.VMEM((BLOCK, HALF_COLS), BF16),
            pltpu.VMEM((8, BLOCK), F32),
            pltpu.VMEM((8, BLOCK), F32),
            pltpu.VMEM((HQ, HEAD), F32),
            pltpu.VMEM((2, HALF_HEADS, HEAD), BF16),
            pltpu.VMEM((N, HALF_HEADS, HEAD), BF16),
            pltpu.VMEM((HEAD, HEAD), BF16),
            pltpu.VMEM((HEAD, HEAD), BF16),
            pltpu.VMEM((2, HALF_KV, RB, HEAD), BF16),
            pltpu.VMEM((2, HALF_KV, 2, BLOCK), F32),
            pltpu.VMEM((2, CHIPS, RB, HEAD), BF16),
            pltpu.VMEM((2, CHIPS, 2, BLOCK), F32),
            pltpu.VMEM((2, 2 * HEAD, HALF_D), BF16),
            pltpu.VMEM((2, GROUPS, SB, N, HEAD), BF16),
            pltpu.VMEM((CHIPS, 2, GROUPS, N, HEAD), BF16),
            pltpu.VMEM((D // HEAD, HEAD), F32),
            pltpu.VMEM((D // HEAD, HEAD), F32),
            pltpu.SMEM((1,), jnp.int32),
            pltpu.SMEM((1,), jnp.int32),
            dma((12,)),
            dma,
            dma((2,)),
            dma((4,)),
            dma((4,)),
            dma((2,)),
            dma((2,)),
            dma((2,)),
            dma((2,)),
            dma((2, GROUPS)),
            dma,
        ],
        compiler_params=pltpu.CompilerParams(collective_id=0, has_side_effects=True),
        name="decode_step",
    )(
        query_new,
        key_new,
        value_new,
        prefix_keys,
        prefix_values,
        sample_suffix_keys,
        sample_suffix_values,
        prefix_len,
        suffix_len,
        residual,
        out_weight,
        norm_gain,
    )
    return hidden.reshape(1, D), normed.reshape(1, D)


def solution(mesh):
    placed = (
        P(("dp", "mp"), None),
        P(("dp", "mp"), None),
        P(("dp", "mp"), None),
        P(("dp", "mp"), None),
        P(("dp", "mp"), None),
        P(("dp", "mp"), None, None),
        P(("dp", "mp"), None, None),
        P("dp"),
        P(("dp", "mp")),
        P(("dp", "mp"), None),
        P("mp", None),
        P(),
    )
    return jax.shard_map(
        local,
        mesh=mesh,
        in_specs=placed,
        out_specs=(P(("dp", "mp"), None), P(("dp", "mp"), None)),
        check_vma=False,
    )
```

time: 36.9 us -> 31.8 us (0.86)
  Pallas kernels: 31.9 us -> 29 us
  local copies, waits for them, and re-layouts: 2.76 us -> 0.68 us
    pallas_call x1, Pallas kernels: 31.9 us -> 29 us  [local(): pl.pallas_call(kernel, out_shape=(pltpu.VMEM((D // HEAD, HEAD), BF16), pl...]
    reshape x1 -> x0, local copies, waits for them, and re-layouts: 1.35 us -> none  [local(): norm_gain.reshape(1, D)]
    reshape x1, local copies, waits for them, and re-layouts: 1.41 us -> 0.68 us  [local(): return (hidden.reshape(1, D), normed.reshape(1, D))]
where the time goes in v2:
time: 31.8 us; the launch traced here: 31.6 us
  Pallas kernels  29 us (91%)
  between operations  1.93 us (6%)
  local copies, waits for them, and re-layouts  0.68 us (2%)
    pallas_call x1, Pallas kernels, local(): pl.pallas_call(kernel, out_shape=(pltpu.VMEM((D // HEAD, HEAD), BF16), pl...  29 us
    reshape x1, local copies, waits for them, and re-layouts, local(): return (hidden.reshape(1, D), normed.reshape(1, D))  0.68 us

profile of v2, /device:TPU:1, one launch (start us, length us, event | category | flops | bytes accessed | tf_op | source)
XLA Modules:
  0.0 31.6 jit_solution(17783664059328597671)
XLA Ops:
  1.9 29.0 %decode_step.1 = (bf16[64,128]{1,0:T(8,128)(2,1)S(1)}, bf16[64,128]{1,0:T(8,128)(2,1)S(1)}) custom-call(bf16[1,4096]{1,0:T(2,128)(2,1)} %q_hbm.1, bf16[1,1024]{1,0:T(2,128)(2,1)} %kn_hbm.1, bf16[1,1024]{1,0:T(2,128)(2,1)} %vn_hbm.1, bf16[128,1024]{1,0:T(8,128)(2,1)} %pk_hbm.1, bf16[128,1024]{1,0:T(8,128)(2,1)} %pv_hbm.1, bf16[1,64,1024]{2,1,0:T(8,128)(2,1)} %sk_hbm.1, ...), custom_call_target="tpu_custom_call" | custom-call | tf_op jit(solution)/shard_map/decode_step/pallas_call | solution.py:401
  31.0 0.7 %copy_bitcast_fusion = (bf16[1,8192]{1,0:T(2,128)(2,1)}, bf16[1,8192]{1,0:T(2,128)(2,1)}) fusion(bf16[1,1,64,128]{3,2,1,0:T(8,128)(2,1)S(1)} %bitcast.9, bf16[1,1,64,128]{3,2,1,0:T(8,128)(2,1)S(1)} %bitcast.8), kind=kLoop, calls=%fused_computation | loop fusion | bytes 65536 | tf_op jit(solution)/shard_map/reshape | solution.py:465

commit v3 on v2

--- a/solution.py
+++ b/solution.py
@@ -26,7 +26,9 @@
 F32 = jnp.float32
 BF16 = jnp.bfloat16
 HALF_CHIPS = CHIPS // 2
-SB = N // 2
+BATCHES = ((0, 4), (4, 4), (8, 8))
+NB = len(BATCHES)
+SB = 8
 RB = 4 * SB
 
 
@@ -97,7 +99,7 @@
     c = me % 2
     p = 1 - c
     partner = z * 2 + p
-    my_batch = z // HALF_CHIPS
+    my_batch = z // 2 - z // 6
 
     def at_mp(index):
         return {"mp": index}
@@ -143,22 +145,24 @@
     with jax.named_scope("prep"):
         barrier = pltpu.get_barrier_semaphore()
 
-        def greet(step, carry):
-            pl.semaphore_signal(
-                barrier,
-                inc=1,
-                device_id=at_mp((me + step) % N),
-                device_id_type=pl.DeviceIdType.MESH,
-            )
-            return carry
-
-        lax.fori_loop(1, N, greet, 0)
+        for step in (4, 3, 5, 2, 6, 1, 7):
+            for half in (0, 1):
+                pl.semaphore_signal(
+                    barrier,
+                    inc=1,
+                    device_id=at_mp(((z + step) % CHIPS) * 2 + half),
+                    device_id_type=pl.DeviceIdType.MESH,
+                )
+        pl.semaphore_signal(
+            barrier, inc=1, device_id=at_mp(partner), device_id_type=pl.DeviceIdType.MESH
+        )
         for copy in local:
             copy.start()
 
         rows = lax.broadcasted_iota(jnp.int32, (HEAD, HEAD), 0)
         cols = lax.broadcasted_iota(jnp.int32, (HEAD, HEAD), 1)
-        to_heads[...] = jnp.where(cols == (rows % SB) * N + rows // SB, 1.0, 0.0).astype(BF16)
+        for i, ns in enumerate((4, 8)):
+            to_heads[i] = jnp.where(cols == (rows % ns) * N + rows // ns, 1.0, 0.0).astype(BF16)
         to_samples[...] = jnp.where(cols == (rows % N) * SB + rows // N, 1.0, 0.0).astype(BF16)
         local[10].wait()
         local[11].wait()
@@ -222,48 +226,70 @@
             copy.wait_recv()
 
     scale = HEAD ** (-0.5)
-    row32 = lax.broadcasted_iota(jnp.int32, (RB, BLOCK), 0)
-    col32 = lax.broadcasted_iota(jnp.int32, (RB, BLOCK), 1)
-    diagonal = col32 % RB == row32
+
+    def diagonal(ns):
+        rows = lax.broadcasted_iota(jnp.int32, (4 * ns, 32 * ns), 0)
+        cols = lax.broadcasted_iota(jnp.int32, (4 * ns, 32 * ns), 1)
+        return cols % (4 * ns) == rows
 
     def attend(b):
+        start, ns = BATCHES[b]
+        rb = 4 * ns
         with jax.named_scope("qwait%d" % b):
-            wait_bytes(qbuf.at[pl.ds(SB * b, SB)], qr_sem.at[b])
+            wait_bytes(qbuf.at[pl.ds(start, ns)], qr_sem.at[b])
         with jax.named_scope("attn%d" % b):
+            size = ns * HALF_HEADS
             queries = nn(
-                to_heads[...], qbuf[SB * b : SB * (b + 1)].reshape(SB * HALF_HEADS, HEAD)
+                to_heads[ns // 8, 0:size, 0:size],
+                qbuf[start : start + ns].reshape(size, HEAD),
             ).astype(BF16)
-            shown_own = (col32 < PRE_DEV) | (row32 % SB + SB * b == me)
-            shown_par = (col32 < PRE_DEV) | (row32 % SB + SB * b == partner)
-            bias_own = jnp.where(shown_own, bias[0:1, :], NEG)
-            bias_par = jnp.where(shown_par, bpar[0:1, :], NEG)
+            sample = lax.broadcasted_iota(jnp.int32, (rb, BLOCK), 0) % ns + start
+            shared = lax.broadcasted_iota(jnp.int32, (rb, BLOCK), 1) < PRE_DEV
+            bias_own = jnp.where(shared | (sample == me), bias[0:1, :], NEG)
+            bias_par = jnp.where(shared | (sample == partner), bpar[0:1, :], NEG)
+            scores = []
             for j in range(HALF_KV):
-                qj = queries[RB * j : RB * (j + 1), :]
-                own_j = pl.ds(pl.multiple_of(c * HALF_COLS + j * HEAD, HEAD), HEAD)
-                s_own = nt(qj, kfull[:, own_j]) * scale + bias_own
-                s_par = nt(qj, kpar[:, j * HEAD : (j + 1) * HEAD]) * scale + bias_par
-                top = jnp.max(jnp.maximum(s_own, s_par), axis=1, keepdims=True)
-                w_own = jnp.exp(s_own - top)
-                w_par = jnp.exp(s_par - top)
-                total = jnp.sum(w_own + w_par, axis=1, keepdims=True)
-                out = nn(w_own.astype(BF16), vfull[:, own_j]) + nn(
+                qj = queries[rb * j : rb * (j + 1), :]
+                at_own = pl.ds(pl.multiple_of(c * HALF_COLS + j * HEAD, HEAD), HEAD)
+                scores.append(
+                    (
+                        nt(qj, kfull[:, at_own]) * scale + bias_own,
+                        nt(qj, kpar[:, j * HEAD : (j + 1) * HEAD]) * scale + bias_par,
+                    )
+                )
+            tops = [jnp.max(jnp.maximum(x, y), axis=1, keepdims=True) for x, y in scores]
+            weights = [(jnp.exp(x - t), jnp.exp(y - t)) for (x, y), t in zip(scores, tops)]
+            totals = [jnp.sum(x + y, axis=1, keepdims=True) for x, y in weights]
+            for j in range(HALF_KV):
+                at_own = pl.ds(pl.multiple_of(c * HALF_COLS + j * HEAD, HEAD), HEAD)
+                w_own, w_par = weights[j]
+                out = nn(w_own.astype(BF16), vfull[:, at_own]) + nn(
                     w_par.astype(BF16), vpar[:, j * HEAD : (j + 1) * HEAD]
                 )
-                ostage[b, j] = out.astype(BF16)
-                sstage[b, j, 0:1, :] = jnp.sum(
-                    jnp.where(diagonal, top, 0.0), axis=0, keepdims=True
-                )
-                sstage[b, j, 1:2, :] = jnp.sum(
-                    jnp.where(diagonal, total, 0.0), axis=0, keepdims=True
-                )
+                ostage[b, j, 0:rb, :] = out.astype(BF16)
+            for j in range(HALF_KV):
+                for i, stat in enumerate((tops[j], totals[j])):
+                    sstage[b, j, i : i + 1, 0 : 8 * rb] = jnp.sum(
+                        jnp.where(diagonal(ns), stat, 0.0), axis=0, keepdims=True
+                    )
         with jax.named_scope("osend%d" % b):
             for i in (1, 2, 3, 0):
                 j = (z + i) % HALF_CHIPS
                 for half in range(2):
                     target = (HALF_CHIPS * c + j) * 2 + half
                     pairs = (
-                        (ostage.at[b, j], obuf.at[b, z], os_sem.at[b], or_sem.at[b]),
-                        (sstage.at[b, j], sbuf.at[b, z], ss_sem.at[b], sr_sem.at[b]),
+                        (
+                            ostage.at[b, j, pl.ds(0, rb)],
+                            obuf.at[b, z, pl.ds(0, rb)],
+                            os_sem.at[b],
+                            or_sem.at[b],
+                        ),
+                        (
+                            sstage.at[b, j, :, pl.ds(0, 8 * rb)],
+                            sbuf.at[b, z, :, pl.ds(0, 8 * rb)],
+                            ss_sem.at[b],
+                            sr_sem.at[b],
+                        ),
                     )
                     if i:
                         for src, dst, ssem, rsem in pairs:
@@ -281,27 +307,31 @@
                             pltpu.make_async_copy(src, dst, rsem).start()
 
     def project(b):
+        start, ns = BATCHES[b]
+        rb = 4 * ns
         with jax.named_scope("owait%d" % b):
-            wait_bytes(obuf.at[b], or_sem.at[b])
-            wait_bytes(sbuf.at[b], sr_sem.at[b])
+            wait_bytes(obuf.at[b, :, pl.ds(0, rb)], or_sem.at[b])
+            wait_bytes(sbuf.at[b, :, :, pl.ds(0, 8 * rb)], sr_sem.at[b])
         with jax.named_scope("combine%d" % b):
-            stats = sbuf[b]
-            group = lax.broadcasted_iota(jnp.int32, (1, BLOCK), 1) // RB
+            stats = sbuf[b, :, :, 0 : 8 * rb]
+            group = lax.broadcasted_iota(jnp.int32, (1, 8 * rb), 1) // rb
             most = stats[0, 0:1, :]
             for src_z in range(1, CHIPS):
                 most = jnp.maximum(most, stats[src_z, 0:1, :])
-            summed = jnp.zeros((1, BLOCK), F32)
-            factor = jnp.zeros((1, BLOCK), F32)
+            summed = jnp.zeros((1, 8 * rb), F32)
+            factor = jnp.zeros((1, 8 * rb), F32)
             for src_z in range(CHIPS):
                 f = jnp.exp(stats[src_z, 0:1, :] - most)
                 summed = summed + f * stats[src_z, 1:2, :]
                 factor = jnp.where(group == src_z, f, factor)
-            mix = jnp.where(diagonal, factor / summed, 0.0)
+            mix = jnp.where(diagonal(ns), factor / summed, 0.0)
             high = mix.astype(BF16)
             low = (mix - high.astype(F32)).astype(BF16)
-            parts = obuf[b].reshape(CHIPS * RB, HEAD)
+            parts = obuf[b, :, 0:rb, :].reshape(CHIPS * rb, HEAD)
             attn = nn(high, parts) + nn(low, parts)
-            attn = jnp.concatenate([attn[SB * h : SB * (h + 1), :] for h in range(4)], axis=1)
+            attn = jnp.concatenate([attn[ns * h : ns * (h + 1), :] for h in range(4)], axis=1)
+            if ns < SB:
+                attn = jnp.concatenate([attn, jnp.zeros((SB - ns, 4 * HEAD), F32)], axis=0)
             attn = attn.astype(BF16)
         if b == 0:
             with jax.named_scope("waitw"):
@@ -319,7 +349,7 @@
             with jax.named_scope("ysend%d%d" % (b, g)):
 
                 def send_projection(t, carry):
-                    target = SB * b + t
+                    target = start + t
 
                     @pl.when(target != me)
                     def _():
@@ -335,30 +365,26 @@
 
                     return carry
 
-                lax.fori_loop(0, SB, send_projection, 0)
-
-    attend(0)
-    attend(1)
-    project(0)
-    project(1)
+                lax.fori_loop(0, ns, send_projection, 0)
+
+    for b in range(NB):
+        attend(b)
+    for b in range(NB):
+        project(b)
 
     with jax.named_scope("sendwait"):
         wait_bytes(qbuf.at[pl.ds(0, N - 1)], qs_sem)
         for copy in swaps:
             copy.wait_send()
 
-        for b in range(2):
+        for b, (start, ns) in enumerate(BATCHES):
             own_chip = z // HALF_CHIPS == c
-
-            @pl.when(own_chip)
-            def _():
-                wait_bytes(obuf.at[b, pl.ds(0, CHIPS - 1)], os_sem.at[b])
-                wait_bytes(sbuf.at[b, pl.ds(0, CHIPS - 1)], ss_sem.at[b])
-
-            @pl.when(jnp.logical_not(own_chip))
-            def _():
-                wait_bytes(obuf.at[b], os_sem.at[b])
-                wait_bytes(sbuf.at[b], ss_sem.at[b])
+            for here, count in ((own_chip, CHIPS - 1), (jnp.logical_not(own_chip), CHIPS)):
+
+                @pl.when(here)
+                def _():
+                    wait_bytes(obuf.at[b, pl.ds(0, count), pl.ds(0, 4 * ns)], os_sem.at[b])
+                    wait_bytes(sbuf.at[b, pl.ds(0, count), :, pl.ds(0, 32 * ns)], ss_sem.at[b])
 
     with jax.named_scope("ywait"):
         wait_bytes(rbuf, yr_sem)
@@ -369,16 +395,16 @@
         hid_ref[...] = stream.astype(BF16)
         nrm_ref[...] = normed.astype(BF16)
     with jax.named_scope("sendwait2"):
-        for b in range(2):
+        for b, (start, ns) in enumerate(BATCHES):
             for g in range(GROUPS):
 
                 @pl.when(my_batch == b)
                 def _():
-                    wait_bytes(ysend.at[b, g, pl.ds(0, SB - 1)], ys_sem.at[b, g])
+                    wait_bytes(ysend.at[b, g, pl.ds(0, ns - 1)], ys_sem.at[b, g])
 
                 @pl.when(my_batch != b)
                 def _():
-                    wait_bytes(ysend.at[b, g], ys_sem.at[b, g])
+                    wait_bytes(ysend.at[b, g, pl.ds(0, ns)], ys_sem.at[b, g])
 
 
 def local(
@@ -421,14 +447,14 @@
             pltpu.VMEM((HQ, HEAD), F32),
             pltpu.VMEM((2, HALF_HEADS, HEAD), BF16),
             pltpu.VMEM((N, HALF_HEADS, HEAD), BF16),
+            pltpu.VMEM((2, HEAD, HEAD), BF16),
             pltpu.VMEM((HEAD, HEAD), BF16),
-            pltpu.VMEM((HEAD, HEAD), BF16),
-            pltpu.VMEM((2, HALF_KV, RB, HEAD), BF16),
-            pltpu.VMEM((2, HALF_KV, 2, BLOCK), F32),
-            pltpu.VMEM((2, CHIPS, RB, HEAD), BF16),
-            pltpu.VMEM((2, CHIPS, 2, BLOCK), F32),
+            pltpu.VMEM((NB, HALF_KV, RB, HEAD), BF16),
+            pltpu.VMEM((NB, HALF_KV, 2, BLOCK), F32),
+            pltpu.VMEM((NB, CHIPS, RB, HEAD), BF16),
+            pltpu.VMEM((NB, CHIPS, 2, BLOCK), F32),
             pltpu.VMEM((2, 2 * HEAD, HALF_D), BF16),
-            pltpu.VMEM((2, GROUPS, SB, N, HEAD), BF16),
+            pltpu.VMEM((NB, GROUPS, SB, N, HEAD), BF16),
             pltpu.VMEM((CHIPS, 2, GROUPS, N, HEAD), BF16),
             pltpu.VMEM((D // HEAD, HEAD), F32),
             pltpu.VMEM((D // HEAD, HEAD), F32),
@@ -436,14 +462,14 @@
             pltpu.SMEM((1,), jnp.int32),
             dma((12,)),
             dma,
-            dma((2,)),
+            dma((NB,)),
             dma((4,)),
             dma((4,)),
-            dma((2,)),
-            dma((2,)),
-            dma((2,)),
-            dma((2,)),
-            dma((2, GROUPS)),
+            dma((NB,)),
+            dma((NB,)),
+            dma((NB,)),
+            dma((NB,)),
+            dma((NB, GROUPS)),
             dma,
         ],
         compiler_params=pltpu.CompilerParams(collective_id=0, has_side_effects=True),

time: 31.8 us -> 30.5 us (0.959)
  the two profiles are of different devices: /device:TPU:1 before, /device:TPU:36 now
where the time goes in v3:
time: 30.5 us; the launch traced here: 30.3 us
  Pallas kernels  27.7 us (91%)
  between operations  1.93 us (6%)
  local copies, waits for them, and re-layouts  0.68 us (2%)
    pallas_call x1, Pallas kernels, local(): pl.pallas_call(kernel, out_shape=(pltpu.VMEM((D // HEAD, HEAD), BF16), pl...  27.7 us
    reshape x1, local copies, waits for them, and re-layouts, local(): return (hidden.reshape(1, D), normed.reshape(1, D))  0.68 us

profile of v3, /device:TPU:36, one launch (start us, length us, event | category | flops | bytes accessed | tf_op | source)
XLA Modules:
  0.0 30.3 jit_solution(1367366428140703637)
XLA Ops:
  1.9 27.7 %decode_step.1 = (bf16[64,128]{1,0:T(8,128)(2,1)S(1)}, bf16[64,128]{1,0:T(8,128)(2,1)S(1)}) custom-call(bf16[1,4096]{1,0:T(2,128)(2,1)} %q_hbm.1, bf16[1,1024]{1,0:T(2,128)(2,1)} %kn_hbm.1, bf16[1,1024]{1,0:T(2,128)(2,1)} %vn_hbm.1, bf16[128,1024]{1,0:T(8,128)(2,1)} %pk_hbm.1, bf16[128,1024]{1,0:T(8,128)(2,1)} %pv_hbm.1, bf16[1,64,1024]{2,1,0:T(8,128)(2,1)} %sk_hbm.1, ...), custom_call_target="tpu_custom_call" | custom-call | tf_op jit(solution)/shard_map/decode_step/pallas_call | solution.py:427
  29.6 0.7 %copy_bitcast_fusion = (bf16[1,8192]{1,0:T(2,128)(2,1)}, bf16[1,8192]{1,0:T(2,128)(2,1)}) fusion(bf16[1,1,64,128]{3,2,1,0:T(8,128)(2,1)S(1)} %bitcast.9, bf16[1,1,64,128]{3,2,1,0:T(8,128)(2,1)S(1)} %bitcast.8), kind=kLoop, calls=%fused_computation | loop fusion | bytes 65536 | tf_op jit(solution)/shard_map/reshape | solution.py:491

commit v4 on v3

--- a/solution.py
+++ b/solution.py
@@ -20,8 +20,6 @@
 BLOCK = 256
 HALF_COLS = HALF_KV * HEAD
 HALF_D = D // 2
-GROUPS = 2
-GROUP_COLS = HALF_D // GROUPS
 NEG = -1e30
 F32 = jnp.float32
 BF16 = jnp.bfloat16
@@ -82,16 +80,12 @@
     gain64,
     plen_ref,
     slen_ref,
+    bytes_ref,
     loc_sem,
-    qs_sem,
+    send_sem,
     qr_sem,
-    xs_sem,
     xr_sem,
-    os_sem,
     or_sem,
-    ss_sem,
-    sr_sem,
-    ys_sem,
     yr_sem,
 ):
     me = lax.axis_index("mp")
@@ -99,47 +93,51 @@
     c = me % 2
     p = 1 - c
     partner = z * 2 + p
+    own_half = p
+    par_half = c
     my_batch = z // 2 - z // 6
 
     def at_mp(index):
         return {"mp": index}
 
-    def remote(src, dst, ssem, rsem, index):
+    def remote(src, dst, rsem, index):
         return pltpu.make_async_remote_copy(
             src_ref=src,
             dst_ref=dst,
-            send_sem=ssem,
+            send_sem=send_sem,
             recv_sem=rsem,
             device_id=at_mp(index),
             device_id_type=pl.DeviceIdType.MESH,
         )
 
+    def wait_total(size, sem):
+        wait_bytes(bytes_ref.at[pl.ds(0, size // (4 * HEAD))], sem)
+
     def wait_bytes(ref, sem):
         pltpu.make_async_copy(ref, ref, sem).wait()
 
-    own_cols = pl.ds(pl.multiple_of(c * HALF_COLS, HALF_COLS), HALF_COLS)
-    par_cols = pl.ds(pl.multiple_of(p * HALF_COLS, HALF_COLS), HALF_COLS)
+    par_cols = pl.ds(pl.multiple_of(par_half * HALF_COLS, HALF_COLS), HALF_COLS)
     own_d = pl.ds(pl.multiple_of(c * HALF_D, HALF_D), HALF_D)
     par_d = pl.ds(pl.multiple_of(p * HALF_D, HALF_D), HALF_D)
     swaps = [
-        remote(kfull.at[:, par_cols], kpar, xs_sem.at[0], xr_sem.at[0], partner),
-        remote(vfull.at[:, par_cols], vpar, xs_sem.at[1], xr_sem.at[1], partner),
-        remote(bias, bpar, xs_sem.at[2], xr_sem.at[2], partner),
-        remote(w_hbm.at[:, par_d], wbuf.at[c], xs_sem.at[3], xr_sem.at[3], partner),
+        remote(kfull.at[:, par_cols], kpar, xr_sem.at[0], partner),
+        remote(vfull.at[:, par_cols], vpar, xr_sem.at[0], partner),
+        remote(bias, bpar, xr_sem.at[0], partner),
+        remote(w_hbm.at[:, par_d], wbuf.at[c], xr_sem.at[1], partner),
     ]
     local = [
         pltpu.make_async_copy(q_hbm, qv, loc_sem.at[0]),
         pltpu.make_async_copy(kn_hbm, knv, loc_sem.at[1]),
-        pltpu.make_async_copy(vn_hbm, vnv, loc_sem.at[2]),
-        pltpu.make_async_copy(pk_hbm, kfull.at[pl.ds(0, PRE_DEV)], loc_sem.at[3]),
-        pltpu.make_async_copy(pv_hbm, vfull.at[pl.ds(0, PRE_DEV)], loc_sem.at[4]),
-        pltpu.make_async_copy(sk_hbm.at[0], kfull.at[pl.ds(PRE_DEV, SUF)], loc_sem.at[5]),
-        pltpu.make_async_copy(sv_hbm.at[0], vfull.at[pl.ds(PRE_DEV, SUF)], loc_sem.at[6]),
-        pltpu.make_async_copy(res_hbm, resv, loc_sem.at[7]),
-        pltpu.make_async_copy(gain_hbm, gainv, loc_sem.at[8]),
-        pltpu.make_async_copy(w_hbm.at[:, own_d], wbuf.at[c], loc_sem.at[9]),
-        pltpu.make_async_copy(plen_hbm, plen_ref, loc_sem.at[10]),
-        pltpu.make_async_copy(slen_hbm, slen_ref, loc_sem.at[11]),
+        pltpu.make_async_copy(vn_hbm, vnv, loc_sem.at[8]),
+        pltpu.make_async_copy(pk_hbm, kfull.at[pl.ds(0, PRE_DEV)], loc_sem.at[2]),
+        pltpu.make_async_copy(pv_hbm, vfull.at[pl.ds(0, PRE_DEV)], loc_sem.at[2]),
+        pltpu.make_async_copy(sk_hbm.at[0], kfull.at[pl.ds(PRE_DEV, SUF)], loc_sem.at[2]),
+        pltpu.make_async_copy(sv_hbm.at[0], vfull.at[pl.ds(PRE_DEV, SUF)], loc_sem.at[2]),
+        pltpu.make_async_copy(res_hbm, resv, loc_sem.at[3]),
+        pltpu.make_async_copy(gain_hbm, gainv, loc_sem.at[4]),
+        pltpu.make_async_copy(w_hbm.at[:, own_d], wbuf.at[c], loc_sem.at[5]),
+        pltpu.make_async_copy(plen_hbm, plen_ref, loc_sem.at[6]),
+        pltpu.make_async_copy(slen_hbm, slen_ref, loc_sem.at[7]),
     ]
 
     with jax.named_scope("prep"):
@@ -200,17 +198,16 @@
             k = i // 2
             half = i % 2
             step = CHIPS // 2 + ((k + 1) // 2) * (1 - 2 * (k % 2))
-            target = ((z + step) % CHIPS) * 2 + half
-            remote(qsend.at[half], qbuf.at[me], qs_sem, qr_sem.at[my_batch], target).start()
+            target = ((z + step) % CHIPS) * 2 + 1 - half
+            remote(qsend.at[half], qbuf.at[me], qr_sem.at[my_batch], target).start()
             return carry
 
         lax.fori_loop(0, N - 2, send_query, 0)
-        remote(qsend.at[p], qbuf.at[me], qs_sem, qr_sem.at[my_batch], partner).start()
-        pltpu.make_async_copy(qsend.at[c], qbuf.at[me], qr_sem.at[my_batch]).start()
+        remote(qsend.at[par_half], qbuf.at[me], qr_sem.at[my_batch], partner).start()
+        pltpu.make_async_copy(qsend.at[own_half], qbuf.at[me], qr_sem.at[my_batch]).start()
 
     with jax.named_scope("kvsend"):
-        for copy in local[3:7]:
-            copy.wait()
+        wait_total(2 * 2 * (PRE_DEV + SUF) * KVH * HEAD, loc_sem.at[2])
         for copy in swaps:
             copy.start()
 
@@ -222,8 +219,7 @@
             gain64[r, :] = gainv[r * HEAD : (r + 1) * HEAD].astype(F32)
 
     with jax.named_scope("kvwait"):
-        for copy in swaps[0:3]:
-            copy.wait_recv()
+        wait_total(2 * 2 * BLOCK * HALF_COLS + 4 * 8 * BLOCK, xr_sem.at[0])
 
     scale = HEAD ** (-0.5)
 
@@ -231,6 +227,9 @@
         rows = lax.broadcasted_iota(jnp.int32, (4 * ns, 32 * ns), 0)
         cols = lax.broadcasted_iota(jnp.int32, (4 * ns, 32 * ns), 1)
         return cols % (4 * ns) == rows
+
+    def sums_bytes(ns):
+        return 2 * 4 * ns * HEAD + 4 * 2 * 32 * ns
 
     def attend(b):
         start, ns = BATCHES[b]
@@ -250,7 +249,7 @@
             scores = []
             for j in range(HALF_KV):
                 qj = queries[rb * j : rb * (j + 1), :]
-                at_own = pl.ds(pl.multiple_of(c * HALF_COLS + j * HEAD, HEAD), HEAD)
+                at_own = pl.ds(pl.multiple_of(own_half * HALF_COLS + j * HEAD, HEAD), HEAD)
                 scores.append(
                     (
                         nt(qj, kfull[:, at_own]) * scale + bias_own,
@@ -261,7 +260,7 @@
             weights = [(jnp.exp(x - t), jnp.exp(y - t)) for (x, y), t in zip(scores, tops)]
             totals = [jnp.sum(x + y, axis=1, keepdims=True) for x, y in weights]
             for j in range(HALF_KV):
-                at_own = pl.ds(pl.multiple_of(c * HALF_COLS + j * HEAD, HEAD), HEAD)
+                at_own = pl.ds(pl.multiple_of(own_half * HALF_COLS + j * HEAD, HEAD), HEAD)
                 w_own, w_par = weights[j]
                 out = nn(w_own.astype(BF16), vfull[:, at_own]) + nn(
                     w_par.astype(BF16), vpar[:, j * HEAD : (j + 1) * HEAD]
@@ -276,42 +275,34 @@
             for i in (1, 2, 3, 0):
                 j = (z + i) % HALF_CHIPS
                 for half in range(2):
-                    target = (HALF_CHIPS * c + j) * 2 + half
+                    target = (HALF_CHIPS * own_half + j) * 2 + half
                     pairs = (
-                        (
-                            ostage.at[b, j, pl.ds(0, rb)],
-                            obuf.at[b, z, pl.ds(0, rb)],
-                            os_sem.at[b],
-                            or_sem.at[b],
-                        ),
+                        (ostage.at[b, j, pl.ds(0, rb)], obuf.at[b, z, pl.ds(0, rb)]),
                         (
                             sstage.at[b, j, :, pl.ds(0, 8 * rb)],
                             sbuf.at[b, z, :, pl.ds(0, 8 * rb)],
-                            ss_sem.at[b],
-                            sr_sem.at[b],
                         ),
                     )
                     if i:
-                        for src, dst, ssem, rsem in pairs:
-                            remote(src, dst, ssem, rsem, target).start()
+                        for src, dst in pairs:
+                            remote(src, dst, or_sem.at[b], target).start()
                         continue
 
                     @pl.when(target != me)
                     def _():
-                        for src, dst, ssem, rsem in pairs:
-                            remote(src, dst, ssem, rsem, target).start()
+                        for src, dst in pairs:
+                            remote(src, dst, or_sem.at[b], target).start()
 
                     @pl.when(target == me)
                     def _():
-                        for src, dst, ssem, rsem in pairs:
-                            pltpu.make_async_copy(src, dst, rsem).start()
+                        for src, dst in pairs:
+                            pltpu.make_async_copy(src, dst, or_sem.at[b]).start()
 
     def project(b):
         start, ns = BATCHES[b]
         rb = 4 * ns
         with jax.named_scope("owait%d" % b):
-            wait_bytes(obuf.at[b, :, pl.ds(0, rb)], or_sem.at[b])
-            wait_bytes(sbuf.at[b, :, :, pl.ds(0, 8 * rb)], sr_sem.at[b])
+            wait_total(CHIPS * sums_bytes(ns), or_sem.at[b])
         with jax.named_scope("combine%d" % b):
             stats = sbuf[b, :, :, 0 : 8 * rb]
             group = lax.broadcasted_iota(jnp.int32, (1, 8 * rb), 1) // rb
@@ -337,54 +328,34 @@
             with jax.named_scope("waitw"):
                 local[9].wait()
                 swaps[3].wait_recv()
-        for g in range(GROUPS):
-            with jax.named_scope("proj%d%d" % (b, g)):
-                at = slice(g * GROUP_COLS, (g + 1) * GROUP_COLS)
-                y = nn(attn[:, 0 : 2 * HEAD], wbuf[0, :, at]) + nn(
-                    attn[:, 2 * HEAD : 4 * HEAD], wbuf[1, :, at]
-                )
-                y = jnp.concatenate([y[:, HEAD * i : HEAD * (i + 1)] for i in range(N)], axis=0)
-                y = nn(to_samples[...], y.astype(BF16)).astype(BF16)
-                ysend[b, g] = y.reshape(SB, N, HEAD)
-            with jax.named_scope("ysend%d%d" % (b, g)):
-
-                def send_projection(t, carry):
-                    target = start + t
-
-                    @pl.when(target != me)
-                    def _():
-                        remote(
-                            ysend.at[b, g, t], rbuf.at[z, c, g], ys_sem.at[b, g], yr_sem, target
-                        ).start()
-
-                    @pl.when(target == me)
-                    def _():
-                        pltpu.make_async_copy(
-                            ysend.at[b, g, t], rbuf.at[z, c, g], yr_sem
-                        ).start()
-
-                    return carry
-
-                lax.fori_loop(0, ns, send_projection, 0)
-
-    for b in range(NB):
+        with jax.named_scope("proj%d" % b):
+            y = nn(attn[:, 0 : 2 * HEAD], wbuf[0]) + nn(attn[:, 2 * HEAD : 4 * HEAD], wbuf[1])
+            for g in range(2):
+                part = [y[:, HEAD * i : HEAD * (i + 1)] for i in range(N * g, N * (g + 1))]
+                part = jnp.concatenate(part, axis=0).astype(BF16)
+                part = nn(to_samples[...], part).astype(BF16)
+                ysend[b, :, N * g : N * (g + 1), :] = part.reshape(SB, N, HEAD)
+        with jax.named_scope("ysend%d" % b):
+
+            def send_projection(t, carry):
+                target = start + t
+
+                @pl.when(target != me)
+                def _():
+                    remote(ysend.at[b, t], rbuf.at[z, c], yr_sem, target).start()
+
+                @pl.when(target == me)
+                def _():
+                    pltpu.make_async_copy(ysend.at[b, t], rbuf.at[z, c], yr_sem).start()
+
+                return carry
+
+            lax.fori_loop(0, ns, send_projection, 0)
+
+    for b in (0, 2, 1):
         attend(b)
-    for b in range(NB):
+    for b in (0, 2, 1):
         project(b)
-
-    with jax.named_scope("sendwait"):
-        wait_bytes(qbuf.at[pl.ds(0, N - 1)], qs_sem)
-        for copy in swaps:
-            copy.wait_send()
-
-        for b, (start, ns) in enumerate(BATCHES):
-            own_chip = z // HALF_CHIPS == c
-            for here, count in ((own_chip, CHIPS - 1), (jnp.logical_not(own_chip), CHIPS)):
-
-                @pl.when(here)
-                def _():
-                    wait_bytes(obuf.at[b, pl.ds(0, count), pl.ds(0, 4 * ns)], os_sem.at[b])
-                    wait_bytes(sbuf.at[b, pl.ds(0, count), :, pl.ds(0, 32 * ns)], ss_sem.at[b])
 
     with jax.named_scope("ywait"):
         wait_bytes(rbuf, yr_sem)
@@ -394,17 +365,20 @@
         normed = stream * lax.rsqrt(meansq + 1e-05) * gain64[...]
         hid_ref[...] = stream.astype(BF16)
         nrm_ref[...] = normed.astype(BF16)
-    with jax.named_scope("sendwait2"):
-        for b, (start, ns) in enumerate(BATCHES):
-            for g in range(GROUPS):
-
-                @pl.when(my_batch == b)
-                def _():
-                    wait_bytes(ysend.at[b, g, pl.ds(0, ns - 1)], ys_sem.at[b, g])
-
-                @pl.when(my_batch != b)
-                def _():
-                    wait_bytes(ysend.at[b, g, pl.ds(0, ns)], ys_sem.at[b, g])
+    with jax.named_scope("sendwait"):
+        sent = (N - 1) * 2 * HALF_HEADS * HEAD
+        sent += 2 * 2 * BLOCK * HALF_COLS + 4 * 8 * BLOCK + 2 * 2 * HEAD * HALF_D
+        sent += sum(2 * HALF_CHIPS * sums_bytes(ns) for _, ns in BATCHES)
+        sent += (N - 1) * 2 * HALF_D
+        own_chip = z // HALF_CHIPS == own_half
+
+        @pl.when(own_chip)
+        def _():
+            wait_total(sent - sum(sums_bytes(ns) for _, ns in BATCHES), send_sem)
+
+        @pl.when(jnp.logical_not(own_chip))
+        def _():
+            wait_total(sent, send_sem)
 
 
 def local(
@@ -454,22 +428,18 @@
             pltpu.VMEM((NB, CHIPS, RB, HEAD), BF16),
             pltpu.VMEM((NB, CHIPS, 2, BLOCK), F32),
             pltpu.VMEM((2, 2 * HEAD, HALF_D), BF16),
-            pltpu.VMEM((NB, GROUPS, SB, N, HEAD), BF16),
-            pltpu.VMEM((CHIPS, 2, GROUPS, N, HEAD), BF16),
+            pltpu.VMEM((NB, SB, HALF_D // HEAD, HEAD), BF16),
+            pltpu.VMEM((CHIPS, 2, HALF_D // HEAD, HEAD), BF16),
             pltpu.VMEM((D // HEAD, HEAD), F32),
             pltpu.VMEM((D // HEAD, HEAD), F32),
             pltpu.SMEM((1,), jnp.int32),
             pltpu.SMEM((1,), jnp.int32),
-            dma((12,)),
+            pltpu.VMEM((8192, HEAD), F32),
+            dma((9,)),
             dma,
             dma((NB,)),
-            dma((4,)),
-            dma((4,)),
+            dma((2,)),
             dma((NB,)),
-            dma((NB,)),
-            dma((NB,)),
-            dma((NB,)),
-            dma((NB, GROUPS)),
             dma,
         ],
         compiler_params=pltpu.CompilerParams(collective_id=0, has_side_effects=True),

time: 30.5 us -> 28.8 us (0.944)
  the two profiles are of different devices: /device:TPU:36 before, /device:TPU:1 now
where the time goes in v4:
time: 28.8 us; the launch traced here: 28.6 us
  Pallas kernels  26 us (90%)
  between operations  1.93 us (7%)
  local copies, waits for them, and re-layouts  0.68 us (2%)
    pallas_call x1, Pallas kernels, local(): pl.pallas_call(kernel, out_shape=(pltpu.VMEM((D // HEAD, HEAD), BF16), pl...  26 us
    reshape x1, local copies, waits for them, and re-layouts, local(): return (hidden.reshape(1, D), normed.reshape(1, D))  0.68 us

profile of v4, /device:TPU:1, one launch (start us, length us, event | category | flops | bytes accessed | tf_op | source)
XLA Modules:
  0.0 28.6 jit_solution(5903399680596031376)
XLA Ops:
  1.9 26.0 %decode_step.1 = (bf16[64,128]{1,0:T(8,128)(2,1)S(1)}, bf16[64,128]{1,0:T(8,128)(2,1)S(1)}) custom-call(bf16[1,4096]{1,0:T(2,128)(2,1)} %q_hbm.1, bf16[1,1024]{1,0:T(2,128)(2,1)} %kn_hbm.1, bf16[1,1024]{1,0:T(2,128)(2,1)} %vn_hbm.1, bf16[128,1024]{1,0:T(8,128)(2,1)} %pk_hbm.1, bf16[128,1024]{1,0:T(8,128)(2,1)} %pv_hbm.1, bf16[1,64,1024]{2,1,0:T(8,128)(2,1)} %sk_hbm.1, ...), custom_call_target="tpu_custom_call" | custom-call | tf_op jit(solution)/shard_map/decode_step/pallas_call | solution.py:401
  27.9 0.7 %copy_bitcast_fusion = (bf16[1,8192]{1,0:T(2,128)(2,1)}, bf16[1,8192]{1,0:T(2,128)(2,1)}) fusion(bf16[1,1,64,128]{3,2,1,0:T(8,128)(2,1)S(1)} %bitcast.9, bf16[1,1,64,128]{3,2,1,0:T(8,128)(2,1)S(1)} %bitcast.8), kind=kLoop, calls=%fused_computation | loop fusion | bytes 65536 | tf_op jit(solution)/shard_map/reshape | solution.py:461

commit v5 on v4

--- a/solution.py
+++ b/solution.py
@@ -67,8 +67,7 @@
     q32,
     qsend,
     qbuf,
-    to_heads,
-    to_samples,
+    y32,
     ostage,
     sstage,
     obuf,
@@ -143,12 +142,13 @@
     with jax.named_scope("prep"):
         barrier = pltpu.get_barrier_semaphore()
 
-        for step in (4, 3, 5, 2, 6, 1, 7):
+        for t in range(CHIPS - 1):
+            chip = t + 1 + (t - z) // CHIPS
             for half in (0, 1):
                 pl.semaphore_signal(
                     barrier,
                     inc=1,
-                    device_id=at_mp(((z + step) % CHIPS) * 2 + half),
+                    device_id=at_mp(chip * 2 + half),
                     device_id_type=pl.DeviceIdType.MESH,
                 )
         pl.semaphore_signal(
@@ -157,11 +157,6 @@
         for copy in local:
             copy.start()
 
-        rows = lax.broadcasted_iota(jnp.int32, (HEAD, HEAD), 0)
-        cols = lax.broadcasted_iota(jnp.int32, (HEAD, HEAD), 1)
-        for i, ns in enumerate((4, 8)):
-            to_heads[i] = jnp.where(cols == (rows % ns) * N + rows // ns, 1.0, 0.0).astype(BF16)
-        to_samples[...] = jnp.where(cols == (rows % N) * SB + rows // N, 1.0, 0.0).astype(BF16)
         local[10].wait()
         local[11].wait()
         col = lax.broadcasted_iota(jnp.int32, (8, BLOCK), 1)
@@ -228,6 +223,11 @@
         cols = lax.broadcasted_iota(jnp.int32, (4 * ns, 32 * ns), 1)
         return cols % (4 * ns) == rows
 
+    def regrouped(ns):
+        rows = lax.broadcasted_iota(jnp.int32, (4 * ns, 32 * ns), 0)
+        cols = lax.broadcasted_iota(jnp.int32, (4 * ns, 32 * ns), 1)
+        return cols % (4 * ns) == (rows % ns) * 4 + rows // ns
+
     def sums_bytes(ns):
         return 2 * 4 * ns * HEAD + 4 * 2 * 32 * ns
 
@@ -237,18 +237,18 @@
         with jax.named_scope("qwait%d" % b):
             wait_bytes(qbuf.at[pl.ds(start, ns)], qr_sem.at[b])
         with jax.named_scope("attn%d" % b):
-            size = ns * HALF_HEADS
-            queries = nn(
-                to_heads[ns // 8, 0:size, 0:size],
-                qbuf[start : start + ns].reshape(size, HEAD),
-            ).astype(BF16)
-            sample = lax.broadcasted_iota(jnp.int32, (rb, BLOCK), 0) % ns + start
+            arrived = qbuf[start : start + ns].astype(F32)
+            queries = [
+                jnp.concatenate([arrived[i, 4 * j : 4 * j + 4, :] for i in range(ns)], axis=0)
+                for j in range(HALF_KV)
+            ]
+            sample = lax.broadcasted_iota(jnp.int32, (rb, BLOCK), 0) // 4 + start
             shared = lax.broadcasted_iota(jnp.int32, (rb, BLOCK), 1) < PRE_DEV
             bias_own = jnp.where(shared | (sample == me), bias[0:1, :], NEG)
             bias_par = jnp.where(shared | (sample == partner), bpar[0:1, :], NEG)
             scores = []
             for j in range(HALF_KV):
-                qj = queries[rb * j : rb * (j + 1), :]
+                qj = queries[j].astype(BF16)
                 at_own = pl.ds(pl.multiple_of(own_half * HALF_COLS + j * HEAD, HEAD), HEAD)
                 scores.append(
                     (
@@ -315,7 +315,7 @@
                 f = jnp.exp(stats[src_z, 0:1, :] - most)
                 summed = summed + f * stats[src_z, 1:2, :]
                 factor = jnp.where(group == src_z, f, factor)
-            mix = jnp.where(diagonal(ns), factor / summed, 0.0)
+            mix = jnp.where(regrouped(ns), factor / summed, 0.0)
             high = mix.astype(BF16)
             low = (mix - high.astype(F32)).astype(BF16)
             parts = obuf[b, :, 0:rb, :].reshape(CHIPS * rb, HEAD)
@@ -330,14 +330,14 @@
                 swaps[3].wait_recv()
         with jax.named_scope("proj%d" % b):
             y = nn(attn[:, 0 : 2 * HEAD], wbuf[0]) + nn(attn[:, 2 * HEAD : 4 * HEAD], wbuf[1])
-            for g in range(2):
-                part = [y[:, HEAD * i : HEAD * (i + 1)] for i in range(N * g, N * (g + 1))]
-                part = jnp.concatenate(part, axis=0).astype(BF16)
-                part = nn(to_samples[...], part).astype(BF16)
-                ysend[b, :, N * g : N * (g + 1), :] = part.reshape(SB, N, HEAD)
+            for i in range(HALF_D // HEAD):
+                y32[SB * i : SB * (i + 1), :] = y[:, HEAD * i : HEAD * (i + 1)]
+            for t in range(ns):
+                ysend[b, t] = y32[pl.ds(t, HALF_D // HEAD, stride=SB), :].astype(BF16)
         with jax.named_scope("ysend%d" % b):
 
-            def send_projection(t, carry):
+            def send_projection(i, carry):
+                t = i + 1 - 2 * (i % 2)
                 target = start + t
 
                 @pl.when(target != me)
@@ -354,8 +354,18 @@
 
     for b in (0, 2, 1):
         attend(b)
-    for b in (0, 2, 1):
-        project(b)
+    project(0)
+
+    @pl.when(my_batch < 2)
+    def _():
+        project(2)
+        project(1)
+
+    @pl.when(my_batch == 2)
+    def _():
+        project(1)
+        project(2)
+
 
     with jax.named_scope("ywait"):
         wait_bytes(rbuf, yr_sem)
@@ -421,8 +431,7 @@
             pltpu.VMEM((HQ, HEAD), F32),
             pltpu.VMEM((2, HALF_HEADS, HEAD), BF16),
             pltpu.VMEM((N, HALF_HEADS, HEAD), BF16),
-            pltpu.VMEM((2, HEAD, HEAD), BF16),
-            pltpu.VMEM((HEAD, HEAD), BF16),
+            pltpu.VMEM((SB * HALF_D // HEAD, HEAD), F32),
             pltpu.VMEM((NB, HALF_KV, RB, HEAD), BF16),
             pltpu.VMEM((NB, HALF_KV, 2, BLOCK), F32),
             pltpu.VMEM((NB, CHIPS, RB, HEAD), BF16),

time: 28.8 us -> 28.4 us (0.986)
  Pallas kernels: 26 us -> 25.6 us
    pallas_call x1, Pallas kernels: 26 us -> 25.6 us  [local(): pl.pallas_call(kernel, out_shape=(pltpu.VMEM((D // HEAD, HEAD), BF16), pl...]
where the time goes in v5:
time: 28.4 us; the launch traced here: 28.2 us
  Pallas kernels  25.6 us (90%)
  between operations  1.93 us (7%)
  local copies, waits for them, and re-layouts  0.68 us (2%)
    pallas_call x1, Pallas kernels, local(): pl.pallas_call(kernel, out_shape=(pltpu.VMEM((D // HEAD, HEAD), BF16), pl...  25.6 us
    reshape x1, local copies, waits for them, and re-layouts, local(): return (hidden.reshape(1, D), normed.reshape(1, D))  0.68 us

profile of v5, /device:TPU:1, one launch (start us, length us, event | category | flops | bytes accessed | tf_op | source)
XLA Modules:
  0.0 28.2 jit_solution(12865249445054638239)
XLA Ops:
  1.9 25.6 %decode_step.1 = (bf16[64,128]{1,0:T(8,128)(2,1)S(1)}, bf16[64,128]{1,0:T(8,128)(2,1)S(1)}) custom-call(bf16[1,4096]{1,0:T(2,128)(2,1)} %q_hbm.1, bf16[1,1024]{1,0:T(2,128)(2,1)} %kn_hbm.1, bf16[1,1024]{1,0:T(2,128)(2,1)} %vn_hbm.1, bf16[128,1024]{1,0:T(8,128)(2,1)} %pk_hbm.1, bf16[128,1024]{1,0:T(8,128)(2,1)} %pv_hbm.1, bf16[1,64,1024]{2,1,0:T(8,128)(2,1)} %sk_hbm.1, ...), custom_call_target="tpu_custom_call" | custom-call | tf_op jit(solution)/shard_map/decode_step/pallas_call | solution.py:411
  27.6 0.7 %copy_bitcast_fusion = (bf16[1,8192]{1,0:T(2,128)(2,1)}, bf16[1,8192]{1,0:T(2,128)(2,1)}) fusion(bf16[1,1,64,128]{3,2,1,0:T(8,128)(2,1)S(1)} %bitcast.9, bf16[1,1,64,128]{3,2,1,0:T(8,128)(2,1)S(1)} %bitcast.8), kind=kLoop, calls=%fused_computation | loop fusion | bytes 65536 | tf_op jit(solution)/shard_map/reshape | solution.py:470

commit v6 on v5

--- a/solution.py
+++ b/solution.py
@@ -271,6 +271,9 @@
                     sstage[b, j, i : i + 1, 0 : 8 * rb] = jnp.sum(
                         jnp.where(diagonal(ns), stat, 0.0), axis=0, keepdims=True
                     )
+
+    def send_sums(b):
+        rb = 4 * BATCHES[b][1]
         with jax.named_scope("osend%d" % b):
             for i in (1, 2, 3, 0):
                 j = (z + i) % HALF_CHIPS
@@ -298,7 +301,26 @@
                         for src, dst in pairs:
                             pltpu.make_async_copy(src, dst, or_sem.at[b]).start()
 
-    def project(b):
+    def send_projections(b, low, high):
+        start, ns = BATCHES[b]
+
+        def send_projection(i, carry):
+            t = i + 1 - 2 * (i % 2)
+            target = start + t
+
+            @pl.when(target != me)
+            def _():
+                remote(ysend.at[b, t], rbuf.at[z, c], yr_sem, target).start()
+
+            @pl.when(target == me)
+            def _():
+                pltpu.make_async_copy(ysend.at[b, t], rbuf.at[z, c], yr_sem).start()
+
+            return carry
+
+        lax.fori_loop(low, high, send_projection, 0)
+
+    def project(b, after_first=False):
         start, ns = BATCHES[b]
         rb = 4 * ns
         with jax.named_scope("owait%d" % b):
@@ -324,6 +346,8 @@
             if ns < SB:
                 attn = jnp.concatenate([attn, jnp.zeros((SB - ns, 4 * HEAD), F32)], axis=0)
             attn = attn.astype(BF16)
+        if after_first:
+            send_projections(0, 2, BATCHES[0][1])
         if b == 0:
             with jax.named_scope("waitw"):
                 local[9].wait()
@@ -336,36 +360,17 @@
                 ysend[b, t] = y32[pl.ds(t, HALF_D // HEAD, stride=SB), :].astype(BF16)
         with jax.named_scope("ysend%d" % b):
 
-            def send_projection(i, carry):
-                t = i + 1 - 2 * (i % 2)
-                target = start + t
-
-                @pl.when(target != me)
-                def _():
-                    remote(ysend.at[b, t], rbuf.at[z, c], yr_sem, target).start()
-
-                @pl.when(target == me)
-                def _():
-                    pltpu.make_async_copy(ysend.at[b, t], rbuf.at[z, c], yr_sem).start()
-
-                return carry
-
-            lax.fori_loop(0, ns, send_projection, 0)
-
-    for b in (0, 2, 1):
-        attend(b)
+            send_projections(b, 0, 2 if b == 0 else ns)
+
+    attend(0)
+    send_sums(0)
+    attend(2)
+    attend(1)
+    send_sums(1)
+    send_sums(2)
     project(0)
-
-    @pl.when(my_batch < 2)
-    def _():
-        project(2)
-        project(1)
-
-    @pl.when(my_batch == 2)
-    def _():
-        project(1)
-        project(2)
-
+    project(1, True)
+    project(2)
 
     with jax.named_scope("ywait"):
         wait_bytes(rbuf, yr_sem)

time: 28.4 us -> 28.2 us (level)
  no operation moved by 1% of the time
where the time goes in v6:
time: 28.2 us; the launch traced here: 28 us
  Pallas kernels  25.4 us (90%)
  between operations  1.93 us (7%)
  local copies, waits for them, and re-layouts  0.68 us (2%)
    pallas_call x1, Pallas kernels, local(): pl.pallas_call(kernel, out_shape=(pltpu.VMEM((D // HEAD, HEAD), BF16), pl...  25.4 us
    reshape x1, local copies, waits for them, and re-layouts, local(): return (hidden.reshape(1, D), normed.reshape(1, D))  0.68 us

profile of v6, /device:TPU:1, one launch (start us, length us, event | category | flops | bytes accessed | tf_op | source)
XLA Modules:
  0.0 28.0 jit_solution(2874807452304038527)
XLA Ops:
  1.9 25.4 %decode_step.1 = (bf16[64,128]{1,0:T(8,128)(2,1)S(1)}, bf16[64,128]{1,0:T(8,128)(2,1)S(1)}) custom-call(bf16[1,4096]{1,0:T(2,128)(2,1)} %q_hbm.1, bf16[1,1024]{1,0:T(2,128)(2,1)} %kn_hbm.1, bf16[1,1024]{1,0:T(2,128)(2,1)} %vn_hbm.1, bf16[128,1024]{1,0:T(8,128)(2,1)} %pk_hbm.1, bf16[128,1024]{1,0:T(8,128)(2,1)} %pv_hbm.1, bf16[1,64,1024]{2,1,0:T(8,128)(2,1)} %sk_hbm.1, ...), custom_call_target="tpu_custom_call" | custom-call | tf_op jit(solution)/shard_map/decode_step/pallas_call | solution.py:416
  27.3 0.7 %copy_bitcast_fusion = (bf16[1,8192]{1,0:T(2,128)(2,1)}, bf16[1,8192]{1,0:T(2,128)(2,1)}) fusion(bf16[1,1,64,128]{3,2,1,0:T(8,128)(2,1)S(1)} %bitcast.9, bf16[1,1,64,128]{3,2,1,0:T(8,128)(2,1)S(1)} %bitcast.8), kind=kLoop, calls=%fused_computation | loop fusion | bytes 65536 | tf_op jit(solution)/shard_map/reshape | solution.py:475
